TPU v7x, 128 devices: a whole 4x4x4 slice. The times are simulated.
128 devices in a mesh: rep: 1, dp: 128 (over x, y, z, core).
Axes of the slice: x: 4, y: 4, z: 4, core: 2. Of those that a mesh axis runs over, the one named last changes fastest.
Arguments:
- x: bfloat16 [128, 1024, 1280], P(('rep', 'dp'))
- dy: bfloat16 [128, 1024, 1280], P(('rep', 'dp'))
- w_gate: bfloat16 [2, 1280, 3072], replicated
- w_up: bfloat16 [2, 1280, 3072], replicated
- w_down: bfloat16 [2, 3072, 1280], replicated
- m_w_gate: float32 [2, 1280, 3072], P(None, 'dp')
- m_w_up: float32 [2, 1280, 3072], P(None, 'dp')
- m_w_down: float32 [2, 3072, 1280], P(None, 'dp')
- v_w_gate: float32 [2, 1280, 3072], P(None, 'dp')
- v_w_up: float32 [2, 1280, 3072], P(None, 'dp')
- v_w_down: float32 [2, 3072, 1280], P(None, 'dp')
Outputs:
- output 1: bfloat16 [2, 1280, 3072], P('rep')
- output 2: bfloat16 [2, 1280, 3072], P('rep')
- output 3: bfloat16 [2, 3072, 1280], P('rep')
- output 4: float32 [2, 1280, 3072], P('rep', 'dp')
- output 5: float32 [2, 1280, 3072], P('rep', 'dp')
- output 6: float32 [2, 3072, 1280], P('rep', 'dp')
- output 7: float32 [2, 1280, 3072], P('rep', 'dp')
- output 8: float32 [2, 1280, 3072], P('rep', 'dp')
- output 9: float32 [2, 3072, 1280], P('rep', 'dp')
All inputs are finite; a program needn't handle non-finite values.
Results may differ from a plain program's by a relative error of at most 0.022.
Values are sent between devices in bfloat16 or wider.
A program may use at most 1.5 GiB of HBM per device.

v0:
```python
import jax
import jax.numpy as jnp
from jax import lax

NAMES = ("w_gate", "w_up", "w_down")


def matmul(a, w):
    return jnp.dot(a, w, preferred_element_type=jnp.float32).astype(jnp.bfloat16)


def normed(h):
    wide = h.astype(jnp.float32)
    scale = lax.rsqrt(jnp.mean(wide**2, -1, keepdims=True) + 1e-6)
    return (wide * scale).astype(jnp.bfloat16)


def layer(h, w):
    a = normed(h)
    gate = jnp.dot(a, w["w_gate"], preferred_element_type=jnp.float32)
    up = jnp.dot(a, w["w_up"], preferred_element_type=jnp.float32)
    return h + matmul((jax.nn.silu(gate) * up).astype(jnp.bfloat16), w["w_down"])


def adamw(w, m, v, g):
    m = 0.9 * m + 0.1 * g
    v = 0.95 * v + 0.05 * g * g
    step = m * lax.rsqrt(v + 1e-8) + 0.1 * w
    return (w - 0.02 * step).astype(jnp.bfloat16), m, v


def clipped(gradients, sum_of_squares, count):
    factor = jnp.minimum(1.0, 0.5 * lax.rsqrt(sum_of_squares / count + 1e-30))
    return [g * factor for g in gradients]


def stack(weights, h):
    for number in range(weights["w_gate"].shape[0]):
        h = layer(h, {name: w[number] for name, w in weights.items()})
    return h


def solution(mesh):
    groups = mesh.shape["rep"]

    def step(x, dy, *arrays):
        weights, m, v = (arrays[i : i + 3] for i in (0, 3, 6))
        x, dy = (t.reshape(groups, -1, *t.shape[1:]) for t in (x, dy))

        def of_a_group(x, dy):
            _, back = jax.vjp(lambda w: stack(w, x), dict(zip(NAMES, weights, strict=True)))
            by_weights = back(dy)[0]
            gradients = [by_weights[name].astype(jnp.float32) for name in NAMES]
            gradients = clipped(gradients, sum(jnp.sum(g * g) for g in gradients), sum(g.size for g in gradients))
            new = [adamw(w.astype(jnp.float32), m, v, g) for w, m, v, g in zip(weights, m, v, gradients, strict=True)]
            return tuple(one[which] for which in range(3) for one in new)

        return tuple(t.reshape(-1, *t.shape[2:]) for t in jax.vmap(of_a_group)(x, dy))

    return step
```

profile of v0, /device:TPU:1, one launch (start us, length us, event | category | flops | bytes accessed | tf_op | source)
XLA Modules:
  0.0 973.5 jit_solution(12496058040124639834)
XLA Ops:
  7.2 2.3 fusion.67
  9.6 11.5 %fusion.39 = f32[1024,3072]{1,0:T(8,128)S(1)} fusion(bf16[2,1280,3072]{2,1,0:T(8,128)(2,1)} %param, bf16[1,1024,1280]{2,1,0:T(8,128)(2,1)} %param.4, f32[1024]{0:T(1024)S(1)} %add_rsqrt_fusion), kind=kOutput, calls=%fused_computation.52 | convolution fusion | flops 8056995840 | bytes 23072768 | tf_op jit(solution)/vmap(jvp())/dot_general | solution.py:20
  21.1 16.1 %fusion.37 = f32[1024,3072]{1,0:T(8,128)S(1)} fusion(bf16[2,1280,3072]{2,1,0:T(8,128)(2,1)} %param.5, bf16[1,1024,1280]{2,1,0:T(8,128)(2,1)} %param.4, f32[1024]{0:T(1024)S(1)} %add_rsqrt_fusion), kind=kOutput, calls=%fused_computation.50 | convolution fusion | flops 8056995840 | bytes 23072768 | tf_op jit(solution)/vmap(jvp())/dot_general | solution.py:21
  37.2 6.7 fusion.52
  43.9 13.3 %fusion.71 = (f32[1024]{0:T(1024)S(1)}, bf16[1,1024,1280]{2,1,0:T(8,128)(2,1)S(1)}) fusion(bf16[1,1024,1280]{2,1,0:T(8,128)(2,1)} %param.4, bf16[1024,3072]{1,0:T(8,128)(2,1)} %fusion.52, bf16[2,3072,1280]{2,1,0:T(8,128)(2,1)} %param.3), kind=kOutput, calls=%fused_computation.82 | convolution fusion | flops 8059616256 | bytes 19402752 | tf_op jit(solution)/vmap(jvp())/dot_general | solution.py:9
  57.3 14.9 %fusion.28 = f32[1024,3072]{1,0:T(8,128)} fusion(bf16[2,1280,3072]{2,1,0:T(8,128)(2,1)} %param, bf16[1,1024,1280]{2,1,0:T(8,128)(2,1)S(1)} %get-tuple-element.32, f32[1024]{0:T(1024)S(1)} %bitcast.335), kind=kOutput, calls=%fused_computation.41 | convolution fusion | flops 8056995840 | bytes 23072768 | tf_op jit(solution)/vmap(jvp())/dot_general | solution.py:20
  72.3 13.5 %fusion.31 = f32[1024,3072]{1,0:T(8,128)} fusion(bf16[2,1280,3072]{2,1,0:T(8,128)(2,1)} %param.5, bf16[1,1024,1280]{2,1,0:T(8,128)(2,1)S(1)} %get-tuple-element.32, f32[1024]{0:T(1024)S(1)} %bitcast.336), kind=kOutput, calls=%fused_computation.44 | convolution fusion | flops 8056995840 | bytes 23072768 | tf_op jit(solution)/vmap(jvp())/dot_general | solution.py:21
  85.8 10.1 %fusion.61 = bf16[1024,3072]{1,0:T(8,128)(2,1)} fusion(bf16[2,3072,1280]{2,1,0:T(8,128)(2,1)S(1)} %bitcast.342, bf16[1,1024,1280]{2,1,0:T(8,128)(2,1)S(1)} %copy-done.4), kind=kOutput, calls=%fused_computation.76 | convolution fusion | flops 8056209408 | bytes 16777216 | tf_op jit(solution)/vmap(transpose(jvp()))/dot_general | solution.py:9
  95.9 17.4 %fusion.74 = bf16[1024,1280]{1,0:T(8,128)(2,1)} fusion(bf16[2,1280,3072]{2,1,0:T(8,128)(2,1)} %param.5, bf16[1024,3072]{1,0:T(8,128)(2,1)} %fusion.61, f32[1024,3072]{1,0:T(8,128)} %fusion.28), kind=kOutput, calls=%fused_computation.85 | convolution fusion | flops 8073248768 | bytes 29360128 | tf_op jit(solution)/vmap(transpose(jvp()))/dot_general | solution.py:21
  113.3 12.4 %fusion.6 = bf16[1024,3072]{1,0:T(8,128)(2,1)S(1)} fusion(f32[1024,3072]{1,0:T(8,128)} %fusion.28, f32[1024,3072]{1,0:T(8,128)} %fusion.31, bf16[1024,3072]{1,0:T(8,128)(2,1)} %fusion.61), kind=kLoop, calls=%fused_computation.11 | loop fusion | flops 37748736 | bytes 37748736
  125.7 16.3 %fusion.73 = (f32[1024]{0:T(1024)S(1)}, bf16[1,1024,1280]{2,1,0:T(8,128)(2,1)}) fusion(bf16[1,1024,1280]{2,1,0:T(8,128)(2,1)} %copy-done.6, bf16[1024,1280]{1,0:T(8,128)(2,1)} %fusion.74, bf16[1024,3072]{1,0:T(8,128)(2,1)S(1)} %fusion.6, bf16[2,1280,3072]{2,1,0:T(8,128)(2,1)} %param), kind=kOutput, calls=%fused_computation.84 | convolution fusion | flops 8059616256 | bytes 22024192 | tf_op jit(solution)/vmap(transpose(jvp()))/dot_general | solution.py:20
  142.0 4.0 fusion.99
  146.1 1.4 copy-done.8
  147.5 11.2 %fusion.154 = f32[1280,3072]{0,1:T(8,128)} fusion(bf16[1024,1280]{1,0:T(8,128)(2,1)S(1)} %fusion.99, bf16[1024,3072]{1,0:T(8,128)(2,1)S(1)} %bitcast.331), kind=kOutput, calls=%fused_computation.172 | convolution fusion | flops 8053063680 | bytes 24641536 | tf_op jit(solution)/vmap(transpose(jvp()))/dot_general | solution.py:9
  158.8 1.7 copy-done.5
  160.4 17.0 %fusion.54 = f32[3072,1280]{1,0:T(8,128)} fusion(f32[1024,3072]{1,0:T(8,128)} %fusion.31, f32[1024,3072]{1,0:T(8,128)} %fusion.28, bf16[1,1024,1280]{2,1,0:T(8,128)(2,1)S(1)} %copy-done.5), kind=kOutput, calls=%fused_computation.70 | convolution fusion | flops 8071938048 | bytes 43515904 | tf_op jit(solution)/vmap(transpose(jvp()))/dot_general | solution.py:9
  177.5 11.6 %fusion.64 = bf16[1024,3072]{1,0:T(8,128)(2,1)S(1)} fusion(bf16[1024,1280]{1,0:T(8,128)(2,1)} %copy-done.8, bf16[2,3072,1280]{2,1,0:T(8,128)(2,1)} %param.3), kind=kOutput, calls=%fused_computation.77 | convolution fusion | flops 8056209408 | bytes 16777216 | tf_op jit(solution)/vmap(transpose(jvp()))/dot_general | solution.py:9
  189.2 2.6 copy-done.17
  191.8 15.1 %fusion.2 = f32[3072,1280]{0,1:T(8,128)} fusion(bf16[1024,3072]{1,0:T(8,128)(2,1)S(1)} %fusion.64, f32[1024,3072]{1,0:T(8,128)} %copy-done, bf16[1,1024,1280]{2,1,0:T(8,128)(2,1)S(1)} %copy-done.3, f32[1024]{0:T(1024)S(1)} %copy-done.16), kind=kOutput, calls=%fused_computation.8 | convolution fusion | flops 8075870208 | bytes 37228544 | tf_op jit(solution)/vmap(transpose(jvp()))/dot_general | solution.py:21
  206.9 18.7 %fusion.10 = f32[3072,1280]{0,1:T(8,128)} fusion(f32[1024,3072]{1,0:T(8,128)} %copy-done, f32[1024,3072]{1,0:T(8,128)} %copy-done.1, bf16[1024,3072]{1,0:T(8,128)(2,1)} %copy-done.17, bf16[1,1024,1280]{2,1,0:T(8,128)(2,1)S(1)} %copy-done.3, f32[1024]{0:T(1024)S(1)} %copy-done.16), kind=kOutput, calls=%fused_computation.15 | convolution fusion | flops 8091598848 | bytes 49811456 | tf_op jit(solution)/vmap(transpose(jvp()))/dot_general | solution.py:20
  225.6 14.8 %fusion.150 = f32[3072,1280]{0,1:T(8,128)} fusion(bf16[1024,3072]{1,0:T(8,128)(2,1)} %copy-done.2, bf16[1,1024,1280]{2,1,0:T(8,128)(2,1)} %copy-done.6, f32[1024]{0:T(1024)S(1)} %bitcast.338), kind=kOutput, calls=%fused_computation.171 | convolution fusion | flops 8056995840 | bytes 24645632 | tf_op jit(solution)/vmap(transpose(jvp()))/dot_general | solution.py:20
  240.4 16.0 %fusion.22 = f32[3072,1280]{0,1:T(8,128)} fusion(bf16[1024,3072]{1,0:T(8,128)(2,1)} %fusion.61, f32[1024,3072]{1,0:T(8,128)} %fusion.28, bf16[1,1024,1280]{2,1,0:T(8,128)(2,1)S(1)} %copy-done.7, f32[1024]{0:T(1024)S(1)} %bitcast.339), kind=kOutput, calls=%fused_computation.37 | convolution fusion | flops 8075870208 | bytes 37228544 | tf_op jit(solution)/vmap(transpose(jvp()))/dot_general | solution.py:21
  256.4 367.9 %all-reduce.17 = (bf16[3072,1280]{0,1:T(8,128)(2,1)}, bf16[3072,1280]{0,1:T(8,128)(2,1)}, bf16[3072,1280]{0,1:T(8,128)(2,1)}, bf16[3072,1280]{0,1:T(8,128)(2,1)}) all-reduce(f32[3072,1280]{0,1:T(8,128)} %fusion.10, f32[3072,1280]{0,1:T(8,128)} %fusion.150, f32[3072,1280]{0,1:T(8,128)} %fusion.2, ...), channel_id=17, replica_groups=mesh['axis_0'=128] {'axis_0'}, use_global_device_ids=true, to_apply=%add.1.clone.clone | all-reduce | flops 15728640 | bytes 94371840
  624.4 1.0 fusion.138
  625.4 0.7 fusion.113
  626.1 1.0 fusion.136
  627.2 0.7 fusion.112
  629.2 0.9 convert_bitcast_fusion.3
  630.1 8.4 reduce-scatter.11.cloned.1.call-done
  638.5 0.9 convert_bitcast_fusion.4
  639.4 0.7 fusion.125
  640.8 64.3 %all-reduce.10 = f32[]{:T(128)} all-reduce(f32[]{:T(128)S(6)} %add.102), channel_id=3, replica_groups=mesh['rep'=1,'dp'=128] {'dp'}, use_global_device_ids=true, to_apply=%region_3.4.clone | all-reduce | flops 1 | bytes 8 | tf_op jit(solution)/vmap()/reduce_sum | solution.py:54
  705.8 1.9 fusion.135
  707.7 0.0 all-gather.12.cloned.1.call-start
  707.7 1.3 fusion.132
  709.0 0.8 copy.13
  709.9 1.3 fusion.133
  711.2 0.8 copy.10
  712.0 0.9 copy.17
  712.9 0.9 copy.19
  713.8 0.9 copy.16
  714.7 0.9 copy.18
  715.6 66.8 %all-gather.14.cloned.1.call-done = bf16[1,2,3072,1280]{3,2,1,0:T(8,128)(2,1)} async-done(((bf16[1,2,24,1280]{3,2,1,0:T(8,128)(2,1)}), bf16[1,2,3072,1280]{3,2,1,0:T(8,128)(2,1)}) %all-gather.14.cloned.1.call-update) | async-done | bytes 15728656 | tf_op jit(solution)/reshape | solution.py:58
  782.3 80.7 %all-gather.12.cloned.1.call-done = bf16[1,2,1280,3072]{3,1,0,2:T(2,128)(2,1)} async-done(((bf16[1,2,10,3072]{3,1,0,2:T(2,128)(2,1)}), bf16[1,2,1280,3072]{3,1,0,2:T(2,128)(2,1)}) %all-gather.12.cloned.1.call-update) | async-done | bytes 15728656 | tf_op jit(solution)/reshape | solution.py:58
  863.0 15.5 %copy.15 = bf16[2,1280,3072]{2,1,0:T(8,128)(2,1)} copy(bf16[2,1280,3072]{2,0,1:T(2,128)(2,1)} %bitcast.328) | data formatting | bytes 31457280
  878.5 65.2 %all-gather.10.cloned.1.call-done = bf16[1,2,1280,3072]{3,1,0,2:T(2,128)(2,1)} async-done(((bf16[1,2,10,3072]{3,1,0,2:T(2,128)(2,1)}), bf16[1,2,1280,3072]{3,1,0,2:T(2,128)(2,1)}) %all-gather.10.cloned.1.call-update) | async-done | bytes 15728656 | tf_op jit(solution)/reshape | solution.py:58
  943.7 17.2 %copy.14 = bf16[2,1280,3072]{2,1,0:T(8,128)(2,1)} copy(bf16[2,1280,3072]{2,0,1:T(2,128)(2,1)} %bitcast.329) | data formatting | bytes 31457280
  960.9 5.8 copy.57
  (70 shorter events, 0.4 us)
Async XLA Ops:
  7.2 622.0 %reduce-scatter.13.cloned.1.call-start = ((), (), s32[]{:S(2)}) async-start(), calls=%async_computation.6 | async-start | bytes 15851520
  9.6 11.6 %copy-start.15 = (f32[1024]{0:T(1024)}, f32[1024]{0:T(1024)S(1)}, u32[]{:S(2)}) copy-start(f32[1024]{0:T(1024)S(1)} %add_rsqrt_fusion) | copy-start | bytes 12292
  21.1 16.1 %copy-start = (f32[1024,3072]{1,0:T(8,128)}, f32[1024,3072]{1,0:T(8,128)S(1)}, u32[]{:S(2)}) copy-start(f32[1024,3072]{1,0:T(8,128)S(1)} %fusion.39) | copy-start | bytes 37748740
  37.2 6.7 copy-start.1
  57.2 15.0 %copy-start.6 = (bf16[1,1024,1280]{2,1,0:T(8,128)(2,1)}, bf16[1,1024,1280]{2,1,0:T(8,128)(2,1)S(1)}, u32[]{:S(2)}) copy-start(bf16[1,1024,1280]{2,1,0:T(8,128)(2,1)S(1)} %get-tuple-element.32) | copy-start | bytes 7864324
  57.3 28.5 %slice-start.6 = ((s8[15728640]{0:T(1024)(128)(4,1)}), s8[4194304]{0:T(1024)(128)(4,1)S(1)}, s32[]{:S(2)}) async-start(s8[15728640]{0:T(1024)(128)(4,1)} %bitcast.341), calls=%async_computation.13 | async-start | bytes 8388608
  57.3 28.5 %slice-start.7 = ((s8[15728640]{0:T(1024)(128)(4,1)}), s8[4194304]{0:T(1024)(128)(4,1)S(1)}, s32[]{:S(2)}) async-start(s8[15728640]{0:T(1024)(128)(4,1)} %bitcast.341), calls=%async_computation.14 | async-start | bytes 8388608
  72.2 13.5 %copy-start.4 = (bf16[1,1024,1280]{2,1,0:T(8,128)(2,1)S(1)}, bf16[1,1024,1280]{2,1,0:T(8,128)(2,1)}, u32[]{:S(2)}) copy-start(bf16[1,1024,1280]{2,1,0:T(8,128)(2,1)} %param.2) | copy-start | bytes 7864324
  72.2 13.6 %slice-start.8 = ((s8[15728640]{0:T(1024)(128)(4,1)}), s8[4194304]{0:T(1024)(128)(4,1)S(1)}, s32[]{:S(2)}) async-start(s8[15728640]{0:T(1024)(128)(4,1)} %bitcast.341), calls=%async_computation.15 | async-start | bytes 8388608
  72.2 13.6 %slice-start.9 = ((s8[15728640]{0:T(1024)(128)(4,1)}), s8[3145728]{0:T(1024)(128)(4,1)S(1)}, s32[]{:S(2)}) async-start(s8[15728640]{0:T(1024)(128)(4,1)} %bitcast.341), calls=%async_computation.16 | async-start | bytes 6291456
  113.3 34.2 %slice-start.4 = ((s8[6291456]{0:T(1024)(128)(4,1)}), s8[4194304]{0:T(1024)(128)(4,1)S(1)}, s32[]{:S(2)}) async-start(s8[6291456]{0:T(1024)(128)(4,1)} %bitcast.330), calls=%async_computation.11 | async-start | bytes 8388608
  125.7 16.3 %copy-start.2 = (bf16[1024,3072]{1,0:T(8,128)(2,1)}, bf16[1024,3072]{1,0:T(8,128)(2,1)S(1)}, u32[]{:S(2)}) copy-start(bf16[1024,3072]{1,0:T(8,128)(2,1)S(1)} %fusion.6) | copy-start | bytes 18874372
  125.7 21.8 %slice-start.5 = ((s8[6291456]{0:T(1024)(128)(4,1)}), s8[2097152]{0:T(1024)(128)(4,1)S(1)}, s32[]{:S(2)}) async-start(s8[6291456]{0:T(1024)(128)(4,1)} %bitcast.330), calls=%async_computation.12 | async-start | bytes 4194304
  146.0 1.5 copy-start.8
  158.7 1.7 copy-start.5
  158.7 479.8 %reduce-scatter.11.cloned.1.call-start = ((), (), s32[]{:S(2)}) async-start(), calls=%async_computation.5 | async-start | bytes 15851520
  177.5 604.9 %all-gather.14.cloned.1.call-start = ((), (), s32[]{:S(2)}) async-start(), calls=%async_computation.4 | async-start | bytes 15851520 | tf_op jit(solution)/reshape | solution.py:58
  177.5 14.3 %copy-start.3 = (bf16[1,1024,1280]{2,1,0:T(8,128)(2,1)S(1)}, bf16[1,1024,1280]{2,1,0:T(8,128)(2,1)}, u32[]{:S(2)}) copy-start(bf16[1,1024,1280]{2,1,0:T(8,128)(2,1)} %param.4) | copy-start | bytes 7864324
  177.5 14.2 %copy-start.16 = (f32[1024]{0:T(1024)S(1)}, f32[1024]{0:T(1024)}, u32[]{:S(2)}) copy-start(f32[1024]{0:T(1024)} %copy-done.15) | copy-start | bytes 12292
  189.2 2.6 copy-start.17
  225.6 14.8 %copy-start.7 = (bf16[1,1024,1280]{2,1,0:T(8,128)(2,1)S(1)}, bf16[1,1024,1280]{2,1,0:T(8,128)(2,1)}, u32[]{:S(2)}) copy-start(bf16[1,1024,1280]{2,1,0:T(8,128)(2,1)} %copy-done.6) | copy-start | bytes 7864324
  256.4 449.4 %copy-start.13 = (f32[2,24,1280]{2,1,0:T(8,128)S(1)}, f32[2,24,1280]{2,1,0:T(8,128)}, u32[]{:S(2)}) copy-start(f32[2,24,1280]{2,1,0:T(8,128)} %param.10) | copy-start | bytes 737284
  256.4 449.4 %copy-start.14 = (f32[2,24,1280]{2,1,0:T(8,128)S(1)}, f32[2,24,1280]{2,1,0:T(8,128)}, u32[]{:S(2)}) copy-start(f32[2,24,1280]{2,1,0:T(8,128)} %param.9) | copy-start | bytes 737284
  256.4 451.3 %copy-start.9 = (f32[2,10,3072]{2,0,1:T(2,128)S(1)}, f32[2,10,3072]{2,0,1:T(2,128)}, u32[]{:S(2)}) copy-start(f32[2,10,3072]{2,0,1:T(2,128)} %param.8) | copy-start | bytes 737284
  256.4 451.3 %copy-start.10 = (f32[2,10,3072]{2,0,1:T(2,128)S(1)}, f32[2,10,3072]{2,0,1:T(2,128)}, u32[]{:S(2)}) copy-start(f32[2,10,3072]{2,0,1:T(2,128)} %param.7) | copy-start | bytes 737284
  256.4 453.5 %copy-start.11 = (f32[2,10,3072]{2,0,1:T(2,128)S(1)}, f32[2,10,3072]{2,0,1:T(2,128)}, u32[]{:S(2)}) copy-start(f32[2,10,3072]{2,0,1:T(2,128)} %param.6) | copy-start | bytes 737284
  256.4 453.5 %copy-start.12 = (f32[2,10,3072]{2,0,1:T(2,128)S(1)}, f32[2,10,3072]{2,0,1:T(2,128)}, u32[]{:S(2)}) copy-start(f32[2,10,3072]{2,0,1:T(2,128)} %param.1) | copy-start | bytes 737284
  707.7 155.3 %all-gather.12.cloned.1.call-start = ((), (), s32[]{:S(2)}) async-start(), calls=%async_computation.3 | async-start | bytes 15851520 | tf_op jit(solution)/reshape | solution.py:58
  709.8 233.8 %all-gather.10.cloned.1.call-start = ((), (), s32[]{:S(2)}) async-start(), calls=%async_computation.2 | async-start | bytes 15851520 | tf_op jit(solution)/reshape | solution.py:58
  943.7 17.2 %slice-start = ((s8[15728640]{0:T(1024)(128)(4,1)}), s8[4194304]{0:T(1024)(128)(4,1)S(1)}, s32[]{:S(2)}) async-start(s8[15728640]{0:T(1024)(128)(4,1)} %bitcast.325), calls=%async_computation.7 | async-start | bytes 8388608
  943.7 17.2 %slice-start.1 = ((s8[15728640]{0:T(1024)(128)(4,1)}), s8[4194304]{0:T(1024)(128)(4,1)S(1)}, s32[]{:S(2)}) async-start(s8[15728640]{0:T(1024)(128)(4,1)} %bitcast.325), calls=%async_computation.8 | async-start | bytes 8388608
  943.7 17.2 %slice-start.2 = ((s8[15728640]{0:T(1024)(128)(4,1)}), s8[4194304]{0:T(1024)(128)(4,1)S(1)}, s32[]{:S(2)}) async-start(s8[15728640]{0:T(1024)(128)(4,1)} %bitcast.325), calls=%async_computation.9 | async-start | bytes 8388608
  943.7 17.3 %slice-start.3 = ((s8[15728640]{0:T(1024)(128)(4,1)}), s8[3145728]{0:T(1024)(128)(4,1)S(1)}, s32[]{:S(2)}) async-start(s8[15728640]{0:T(1024)(128)(4,1)} %bitcast.325), calls=%async_computation.10 | async-start | bytes 6291456
Sparse Core Ops, SparseCore 0:
  158.8 237.6 reduce-scatter.12
  401.5 236.9 reduce-scatter.10
  707.8 74.4 all-gather.13
  785.8 77.1 all-gather.11
  866.4 77.1 all-gather.9
where the time goes:
time: 982 us; the launch traced here: 973 us
  blocking collectives  432 us (44%)
  waiting for transfers between devices  221 us (23%)
  matrix products  218 us (22%)
  local copies, waits for them, and re-layouts  51.5 us (5%)
  other arithmetic  33.8 us (3%)
  between operations  17 us (2%)
    unnamed x1, blocking collectives  368 us
    reshape x3, waiting for transfers between devices, step(): t.reshape(-1, *t.shape[2:])  213 us
    dot_general x5, matrix products, layer(): up = jnp.dot(a, w['w_up'], preferred_element_type=jnp.float32)  78.1 us
    dot_general x5, matrix products, layer(): gate = jnp.dot(a, w['w_gate'], preferred_element_type=jnp.float32)  76.2 us
    reduce_sum x1, blocking collectives, of_a_group(): jnp.sum(g * g)  64.3 us
    dot_general x5, matrix products, matmul(): jnp.dot(a, w, preferred_element_type=jnp.float32).astype(jnp.bfloat16)  63.2 us
    unnamed x63, local copies, waits for them, and re-layouts  47.9 us
    unnamed x6, other arithmetic  23.1 us
  transfers between devices with their start and end apart: 5, of which 4 were waited for; matrix products, arithmetic and copies ran while one was open for 12% of the time, Pallas kernels for 0%

commit v1 on v0

v1 whole, which is shorter than its diff:
```python
import functools

import jax
import jax.numpy as jnp
from jax import lax
from jax.experimental import pallas as pl
from jax.experimental.pallas import tpu as pltpu
from jax.sharding import PartitionSpec as P

BF, F32 = jnp.bfloat16, jnp.float32
T, D, FF = 1024, 1280, 3072
L, RING, PAIR = 2, 4, 2
X, Y, Z, CORE = range(4)
HG, HD = FF // PAIR, D // PAIR
ROWS, DROWS = D // (RING**3 * PAIR), FF // (RING**3 * PAIR)
ZROWS = PAIR * RING * ROWS
PAD = 24
MOST = 67043328
HBM, VM = pl.BlockSpec(memory_space=pltpu.HBM), pl.BlockSpec(memory_space=pltpu.VMEM)
dma, vmem = pltpu.SemaphoreType.DMA, pltpu.VMEM
out = jax.ShapeDtypeStruct


class Place:
    def __init__(self):
        i = lax.axis_index("dp")
        chip, core = lax.div(i, PAIR), lax.rem(i, PAIR)
        self.at = [[lax.div(chip, RING**2)], [lax.rem(lax.div(chip, RING), RING)], [lax.rem(chip, RING)], [core, 1 - core]]
        for steps in self.at[:CORE]:
            steps += [lax.rem(steps[0] + r, RING) for r in range(1, RING)]
        self.peers = {}

    def moved(self, dim, by=1):
        by %= len(self.at[dim])
        if (dim, by) not in self.peers:
            x, y, z, core = (steps[by if d == dim else 0] for d, steps in enumerate(self.at))
            self.peers[dim, by] = {"dp": ((x * RING + y) * RING + z) * PAIR + core}
        return self.peers[dim, by]


def meet(peers):
    barrier = pltpu.get_barrier_semaphore()
    for peer in peers:
        pl.semaphore_signal(barrier, inc=1, device_id=peer)
    pl.semaphore_wait(barrier, len(peers))


def remote(src, dst, send, recv, peer):
    return pltpu.make_async_remote_copy(src, dst, send, recv, device_id=peer)


def up(v):
    return v.astype(F32)


def call(kernel, outs, ins, scratch, name, vmem_limit=MOST, ident=None, out_specs=None, **more):
    return pl.pallas_call(
        kernel,
        out_shape=outs,
        in_specs=ins,
        out_specs=out_specs or [HBM] * len(outs),
        scratch_shapes=scratch,
        compiler_params=pltpu.CompilerParams(collective_id=ident, has_side_effects=ident is not None, vmem_limit_bytes=vmem_limit),
        name=name,
        **more,
    )


class Cut:
    def __init__(self, gate):
        self.gate = gate
        self.units = L * (PAIR if gate else 1)
        self.width = HG // 2 if gate else HD
        self.n, self.rows = (1, ZROWS) if gate else (RING, DROWS)

    def dims(self, s):
        return (s, 1 - s, Z) if self.gate else (Z, s, 1 - s)

    def part(self, s, h, base=0):
        first = 384 if self.gate or s == 0 else 256
        return pl.ds(base + first, self.width - first) if h else pl.ds(base, first)

    def index(self, here, s, dim, r, done, cols):
        at = [here.at[d][r % RING] if d == dim else slice(None) if d in done else here.at[d][0] for d in (X, Y, Z)]
        return (at[X], at[Y]) + ((slice(None),) if self.gate else (at[Z], s)) + (slice(None), cols)


GATE, DOWN = Cut(True), Cut(False)
CUTS = (GATE, DOWN)


def ahead(k):
    return 1 if k in (0, 3, 4) else -1


TILES, HALF = 6, 3
TILE = FF // TILES
TN = (((0,), (0,)), ((), ()))


def dw_kernel(a, dg, du, hid, dy, og, ou, od, va, vb, vh, vy, sd, rd, wd, sg, rg, insem, outsem, dsend, drecv, gsend, grecv):
    here = Place()
    c, other = here.at[CORE][0], here.moved(CORE)
    tile = lambda i, base=0: pl.ds(pl.multiple_of(base + i * TILE, TILE), TILE)
    loads = [pltpu.make_async_copy(dy, vy, insem.at[TILES]), pltpu.make_async_copy(a, va, insem.at[TILES + 1])]
    loads += [pltpu.make_async_copy(hid.at[:, tile(i)], vh.at[:, tile(i)], insem.at[i]) for i in range(TILES)]
    loads += [pltpu.make_async_copy(w, vb.at[i], insem.at[TILES + 2 + i]) for i, w in enumerate((dg, du))]
    for cp in loads:
        cp.start()
    meet([other])

    def dsent(i):
        return remote(sd.at[i], rd.at[i], dsend.at[i], drecv.at[i], other)

    def dout(i):
        return pltpu.make_async_copy(rd.at[i], od.at[tile(i), :], outsem.at[i])

    def dadd(i):
        dsent(i).wait_recv()
        rd[i] = (up(rd[i]) + up(wd[i])).astype(BF)
        dout(i).start()

    for cp in loads[: TILES + 2]:
        cp.wait()

    def dtile(i, _):
        full = lax.dot_general(vh[:, tile(i)], vy[...], TN, preferred_element_type=F32).astype(BF)
        low, high = full[:, :HD], full[:, HD:]
        sd[i] = jnp.where(c == 0, high, low)
        wd[i] = jnp.where(c == 0, low, high)
        dsent(i).start()
        pl.when(i > 0)(lambda: dadd(i - 1))
        return _

    lax.fori_loop(0, TILES, dtile, 0)

    def gsent(w, i):
        return remote(sg.at[w, i], rg.at[w, i], gsend.at[w, i], grecv.at[w, i], other)

    def gout(w, i):
        return pltpu.make_async_copy(rg.at[w, i], (og, ou)[w].at[:, tile(i)], outsem.at[TILES + HALF * w + i])

    for w in range(2):
        loads[TILES + 2 + w].wait()

        def product(i, half):
            cols = tile(i, half * HG)
            return lax.dot_general(va[...], vb[w, :, cols], TN, preferred_element_type=F32).astype(BF)

        def theirs(i, _):
            sg[w, i] = product(i, 1 - c)
            gsent(w, i).start()
            return _

        def mine(i, _):
            own = product(i, c)
            gsent(w, i).wait_recv()
            rg[w, i] = (up(rg[w, i]) + up(own)).astype(BF)
            gout(w, i).start()
            return _

        lax.fori_loop(0, HALF, theirs, 0)
        if w == 0:
            dadd(TILES - 1)
        lax.fori_loop(0, HALF, mine, 0)
    for i in range(TILES):
        dsent(i).wait_send()
        dout(i).wait()
        gsent(i // HALF, i % HALF).wait_send()
        gout(i // HALF, i % HALF).wait()


def dw(a, dg, du, hid, dy):
    tiles = (PAIR, HALF, D, TILE)
    return call(
        dw_kernel, [out((D, HG), BF)] * 2 + [out((FF, HD), BF)], [HBM] * 5,
        [vmem((T, D), BF), vmem((2, T, FF), BF), vmem((T, FF), BF), vmem((T, D), BF)] + [vmem((TILES, TILE, HD), BF)] * 3 + [vmem(tiles, BF)] * 2
        + [dma((TILES + 4,)), dma((2 * TILES,))] + [dma((TILES,))] * 2 + [dma((2, HALF))] * 2,
        "dw", ident=1, cost_estimate=pl.CostEstimate(flops=6 * T * D * FF, bytes_accessed=8 * T * FF, transcendentals=0),
    )(a, dg, du, hid, dy)


PHASES = 3
COPIES = 6


ALL = slice(None)


class Summed:
    def __init__(self, here, cut, src, b, u, s):
        self.here = here
        self.cut, self.src, self.us, self.s, self.dims = cut, src, (u, s), s, cut.dims(s)
        self.got, self.kept = [b[k] for k in ("r1", "r2", "r3")], [b[k] for k in ("o1", "k2", "k3")]
        self.t3, self.sems = b["t3"], (b["send"], b["recv"], b["own"])

    def block(self, phase, r, cols=ALL, first=()):
        dim = self.dims[phase]
        i = self.here.at[dim][r % RING]
        if phase == 2:
            return self.us + first + (i, ALL, cols)
        second = phase == 1 and not self.cut.gate and self.s
        return self.us + first + ((ALL, i) if second else (i, ALL)) + (ALL, cols)

    def first(self, r, h):
        cols = self.cut.part(self.s, h, self.s * self.cut.width if self.cut.gate else 0)
        u = self.us[0]
        return self.src[u if isinstance(u, int) else 0].at[self.cut.index(self.here, self.s, self.dims[0], r, self.dims, cols)]

    def at(self, phase, kind, cols=ALL):
        return self.us + (kind,) + (ALL,) * (PHASES - phase) + (cols,)

    def copy(self, phase, k):
        kind, h = k // 2, k % 2
        cols = self.cut.part(self.s, h)
        got = self.got[phase]
        r = (2, 1 if h else -1, 0)[kind]
        if kind == 2:
            src = got.at[self.at(phase, 0, cols)]
        elif phase == 0:
            src = self.first(r, h)
        elif phase == 1:
            src = self.got[0].at[self.block(1, r, cols, (2,))]
        else:
            src = self.t3.at[self.block(2, r, cols)]
        i = self.us + (phase * COPIES + k,)
        return remote(src, got.at[self.at(phase, kind, cols)], self.sems[0].at[i], self.sems[1].at[i], self.here.moved(self.dims[phase], ahead(k)))

    def own(self, k):
        kind, h = k // 2, k % 2
        src = self.first(0 if kind else ahead(h), h)
        return pltpu.make_async_copy(src, self.kept[0].at[self.at(0, kind, self.cut.part(self.s, h))], self.sems[2].at[self.us + (k,)])

    def start(self):
        for k in range(4):
            self.copy(0, k).start()
        for k in range(4):
            self.own(k).start()

    def pass_on(self, phase):
        got, kept = self.got[phase], self.kept[phase]
        for h in range(2):
            self.copy(phase, h).wait_recv()
            cols = self.cut.part(self.s, h)
            if phase:
                i = self.at(phase, 0, cols)
                got[i] = (up(got[i]) + kept[self.block(phase, ahead(h), cols)]).astype(BF)
            else:
                self.own(h).wait()

                def add(n, _):
                    i = self.us + (0, n, ALL, ALL, cols)
                    got[i] = (up(got[i]) + up(kept[i])).astype(BF)
                    return _

                lax.fori_loop(0, RING, add, 0)
            self.copy(phase, 4 + h).start()

    def finish(self, phase):
        for k in range(2, COPIES):
            self.copy(phase, k).wait_recv()
        got, kept = self.got[phase], self.kept[phase]
        if phase == 0:
            for k in (2, 3):
                self.own(k).wait()

            def add(n, _):
                total = up(kept[self.us + (1, n)]) + up(got[self.us + (2, n)]) + up(got[self.us + (1, n)])
                self.kept[1][self.us + (n,)] = total
                got[self.us + (2, n)] = total.astype(BF)
                return _

            lax.fori_loop(0, RING, add, 0)
        else:
            return kept[self.block(phase, 0)] + up(got[self.us + (2,)]) + up(got[self.us + (1,)])

    def starts(self, phase):
        for k in range(4):
            self.copy(phase, k).start()


def rs_kernel(*refs):
    nu = GATE.units + L
    ins, (og, od, onorm), refs = refs[:nu], refs[nu : nu + 3], list(refs[nu + 3 :])
    names = ("r1", "o1", "k2", "r2", "t3", "k3", "r3", "send", "recv", "own")
    bufs = []
    for _ in CUTS:
        bufs.append(dict(zip(names, refs)))
        del refs[: len(names)]
    f3, f4, ce, cr, co, fd, dr, nb, nr, csend, crecv, nsend, nrecv, putsem = refs
    here = Place()
    c, other = here.at[CORE][0], here.moved(CORE)
    meet([here.moved(d, r) for d in (X, Y, Z) for r in range(1, RING)] + [other])
    srcs = ins[: GATE.units], ins[GATE.units :]

    def streams(g, u):
        return [Summed(here, CUTS[g], srcs[g], bufs[g], u, s) for s in range(2)]

    for u in range(GATE.units):
        for st in streams(0, u) + (streams(1, u) if u < L else []):
            st.start()

    def gate_rows(st):
        f3[0:ZROWS] = st.finish(1)[0]
        for i in range(RING):
            rows = f3[i * PAIR * ROWS : i * PAIR * ROWS + PAD]
            st.kept[2][st.us + (i,)] = rows
            st.t3[st.us + (i,)] = rows.astype(BF)

    def down_rows(st):
        total = st.finish(1)
        st.kept[2][st.us] = total
        st.t3[st.us] = total.astype(BF)

    def swap_g(u):
        return remote(ce.at[u], cr.at[u], csend.at[u], crecv.at[u], other)

    def swap_d(u):
        return remote(fd.at[u, 1 - c], dr.at[u], csend.at[GATE.units + u], crecv.at[GATE.units + u], other)

    def last_g(u):
        for st in streams(0, u):
            f4[0:PAD, pl.ds(st.s * GATE.width, GATE.width)] = st.finish(2)
        low, high = f4[0:16], f4[ROWS : ROWS + 16]
        co[u] = jnp.where(c == 0, low, high).astype(BF)
        ce[u] = jnp.where(c == 0, high, low).astype(BF)
        swap_g(u).start()

    def last_d(u):
        for st in streams(1, u):
            fd[u, st.s] = st.finish(2).astype(BF)
        swap_d(u).start()

    def each(step):
        def both(u, _):
            for g in (1, 0):
                for v in range(CUTS[g].units // L):
                    step(g, u * CUTS[g].units // L + v)
            return _

        lax.fori_loop(0, L, both, 0)

    def all_streams(step):
        each(lambda g, u: [step(g, st) for st in streams(g, u)])

    f3[ZROWS : ZROWS + 8] = jnp.zeros((8, GATE.width), F32)
    f4[PAD : PAD + 8] = jnp.zeros((8, HG), F32)
    all_streams(lambda g, st: st.pass_on(0))
    all_streams(lambda g, st: (st.finish(0), st.starts(1)))
    all_streams(lambda g, st: st.pass_on(1))
    all_streams(lambda g, st: ((gate_rows, down_rows)[g](st), st.starts(2)))
    all_streams(lambda g, st: st.pass_on(2))
    each(lambda g, u: (last_g, last_d)[g](u))

    valid = lax.broadcasted_iota(jnp.int32, (16, HG), 0) < ROWS
    puts = []

    def put(src, dst):
        puts.append(pltpu.make_async_copy(src, dst, putsem.at[len(puts)]))
        puts[-1].start()

    def squares(v):
        v = v * v
        rows = functools.reduce(jnp.add, [v[i : i + 8] for i in range(0, v.shape[0], 8)])
        return functools.reduce(jnp.add, [rows[:, i : i + 128] for i in range(0, v.shape[1], 128)])

    def half(which, n):
        return pl.ds(pl.multiple_of(which * n, 128), n)

    total = jnp.zeros((8, 128), F32)
    for u in range(GATE.units):
        swap_g(u).wait_recv()
        for src, which in ((co, c), (cr, 1 - c)):
            put(src.at[u], og.at[u, :, half(which, HG)])
            total = total + squares(jnp.where(valid, up(src[u]), 0.0))
    for u in range(L):
        swap_d(u).wait_recv()
        for src, i, which in ((fd, (u, c), c), (dr, u, 1 - c)):
            put(src.at[i], od.at[u, :, half(which, HD)])
            total = total + squares(up(src[i]))
    n = 0
    for stage, dim in enumerate((CORE, Z, Y, X)):
        nb[stage] = total
        copies = []
        for r in range(1, PAIR if dim == CORE else RING):
            copies.append(remote(nb.at[stage], nr.at[n], nsend.at[n], nrecv.at[n], here.moved(dim, r)))
            copies[-1].start()
            n += 1
        for i, cp in enumerate(copies):
            cp.wait()
            total = total + nr[n - len(copies) + i]
    nb[4] = total
    put(nb.at[4], onorm)
    for g, cut in enumerate(CUTS):
        for u in range(cut.units):
            for st in streams(g, u):
                for k in range(PHASES * COPIES):
                    st.copy(k // COPIES, k % COPIES).wait_send()
            (swap_g, swap_d)[g](u).wait_send()
    for cp in puts:
        cp.wait()


def rs(gs, ds):
    scratch = []
    for cut in CUTS:
        us = (cut.units, 2)
        block, width = (cut.n, cut.rows, cut.width), cut.width
        scratch += [
            vmem(us + (3, RING) + block, BF), vmem(us + (2, RING) + block, BF), vmem(us + (RING,) + block, F32), vmem(us + (3,) + block, BF),
            vmem(us + (RING, PAD, width), BF), vmem(us + (RING, PAD, width), F32), vmem(us + (3, PAD, width), BF),
            dma(us + (PHASES * COPIES,)), dma(us + (PHASES * COPIES,)), dma(us + (4,)),
        ]
    n = GATE.units + L
    scratch += [vmem((ZROWS + 8, GATE.width), F32), vmem((PAD + 8, HG), F32)] + [vmem((GATE.units, 16, HG), BF)] * 3
    scratch += [vmem((L, 2, DROWS, HD), BF), vmem((L, DROWS, HD), BF), vmem((5, 8, 128), F32), vmem((10, 8, 128), F32)]
    scratch += [dma((n,)), dma((n,)), dma((10,)), dma((10,)), dma((2 * n + 1,))]
    return call(rs_kernel, [out((GATE.units, 16, FF), BF), out((L, DROWS, D), BF), out((8, 128), F32)], [HBM] * n, scratch, "rs", ident=2)(
        *(t.reshape(RING, RING, 1, ZROWS, HG) for t in gs), *(t.reshape(RING, RING, RING, PAIR, DROWS, HD) for t in ds)
    )


COUNT = 3 * L * D * FF


def adamw_kernel(gg, gd, norm, *refs):
    old, (wg, wu, wd), new, (ng, nd, win, wind, sg, sw, sem) = refs[:6], refs[6:9], refs[9:15], refs[15:]
    i = lax.axis_index("dp")
    start, off = pl.multiple_of(i * ROWS // 8 * 8, 8), i * ROWS % 8
    copies = [pltpu.make_async_copy((wg, wu)[u // L].at[u % L, pl.ds(start, 16), :], win.at[u], sem.at[u]) for u in range(GATE.units)]
    copies.append(pltpu.make_async_copy(wd.at[:, pl.ds(pl.multiple_of(i * DROWS, 8), DROWS), :], wind, sem.at[GATE.units]))
    for cp in copies:
        cp.start()
    factor = jnp.minimum(1.0, 0.5 * lax.rsqrt(jnp.full((1, 1), jnp.sum(norm[...])) / COUNT + 1e-30))
    for cp in copies:
        cp.wait()

    def step(k, w, g):
        g = g * factor
        m = 0.9 * old[k][...] + 0.1 * g
        v = 0.95 * old[k + 3][...] + 0.05 * g * g
        new[k][...], new[k + 3][...] = m, v
        return w - 0.02 * (m * lax.rsqrt(v + 1e-8) + 0.1 * w)

    for k in range(2):
        for l in range(L):
            w = up(win[k * L + l])
            rows = w[0:ROWS]
            for skip in (2, 4, 6):
                rows = jnp.where(off == skip, w[skip : skip + ROWS], rows)
            sw[:, l, :] = rows
            sg[:, l, :] = up(gg[k * L + l])[0:ROWS]
        sw[...] = step(k, sw[...], sg[...])
        for l in range(L):
            ng[k * L + l, 0:ROWS] = sw[:, l, :].astype(BF)
    nd[...] = step(2, up(wind[...]), up(gd[...])).astype(BF)


def adamw(gg, gd, norm, moments, weights):
    flip = lambda k, t: t if k % 3 == 2 else jnp.swapaxes(t, 0, 1)
    moments = [flip(k, t) for k, t in enumerate(moments)]
    outs = [out(t.shape, F32) for t in moments] + [out((GATE.units, 16, FF), BF), out((L, DROWS, D), BF)]
    scratch = [vmem((GATE.units, 16, FF), BF), vmem((L, DROWS, D), BF)] + [vmem((ROWS, L, FF), F32)] * 2 + [dma((GATE.units + 1,))]
    *new, ng, nd = call(adamw_kernel, outs, [VM] * 9 + [HBM] * 3, scratch, "adamw", out_specs=[VM] * 8)(gg, gd, norm, *moments, *weights)
    return [flip(k, t) for k, t in enumerate(new)], ng, nd


class Gathered:
    def __init__(self, here, cut, refs, b, u, s):
        self.here, self.cut, self.refs, self.b, self.u, self.s = here, cut, refs, b, u, s
        self.order = cut.dims(s)[::-1]
        n, first = (HG, s * cut.width) if cut.gate else (HD, 0)
        self.whole = [pl.ds(pl.multiple_of(c * n + first, 128), cut.width) for c in here.at[CORE]]

    def ref(self, at):
        return self.refs[self.u // L].at[(self.u % L,) + at]

    def copy(self, phase, k):
        dim, back = self.order[phase], k % 2
        cols = self.whole[0]
        if k >= 2:
            cols = self.cut.part(self.s, back, cols.start)
        v = self.ref(self.cut.index(self.here, self.s, dim, 0 if k < 2 else 2 * back - 1, self.order[:phase], cols))
        i = phase * 4 + k
        return remote(v, v, self.b[0].at[self.u, self.s, i], self.b[1].at[self.u, self.s, i], self.here.moved(dim, 1 - 2 * back))

    def across(self, r, core=0):
        v = self.ref(self.cut.index(self.here, self.s, self.order[2], r, self.order, self.whole[core]))
        i = PHASES * 4 + r % RING
        return remote(v, v, self.b[0].at[self.u, self.s, i], self.b[1].at[self.u, self.s, i], self.here.moved(CORE))

    def start(self, phase):
        for k in range(2):
            self.copy(phase, k).start()
        if phase == 2:
            self.across(0).start()

    def forward(self, phase):
        for k in range(2):
            self.copy(phase, k).wait_recv()
            self.copy(phase, 2 + k).start()
            if phase == 2:
                self.across(2 * k - 1).start()

    def end(self, phase):
        for k in range(2, 4):
            self.copy(phase, k).wait_recv()
        if phase < 2:
            self.start(phase + 1)
        else:
            self.across(2).start()


def ag_kernel(wg, wd, o0, o1, od, cs, cx, zb, zf, zm, csend, crecv, zsend, zrecv, gsend, grecv, dsend, drecv):
    here = Place()
    (x, y, z, c), other = (steps[0] for steps in here.at), here.moved(CORE)
    meet([here.moved(d, r) for d in (X, Y, Z) for r in (1, -1)] + [other])
    half = lambda which, n: pl.ds(pl.multiple_of(which * n, 128), n)
    mine, theirs = c, 1 - c

    def swap_g(u):
        return remote(wg.at[u, :, half(theirs, HG)], cx.at[u], csend.at[u], crecv.at[u], other)

    def swap_d(l, core, which):
        there = od.at[l, x, y, z, core, :, half(which, HD)]
        return remote(wd.at[l, :, half(theirs, HD)], there, csend.at[GATE.units + l], crecv.at[GATE.units + l], other)

    for u in range(GATE.units):
        swap_g(u).start()
    for l in range(L):
        swap_d(l, c, theirs).start()
        od[l, x, y, z, c, :, half(mine, HD)] = wd[l, :, half(mine, HD)]

    def zcopy(s, k):
        back = k % 2
        cols = GATE.part(s, back, s * GATE.width) if k >= 2 else pl.ds(s * GATE.width, GATE.width)
        v = zb.at[here.at[Z][0 if k < 2 else (2 * back - 1) % RING], :, cols]
        return remote(v, v, zsend.at[s, k], zrecv.at[s, k], here.moved(Z, 1 - 2 * back))

    for u in range(GATE.units):
        swap_g(u).wait_recv()
        own, got = up(wg[u, :, half(mine, HG)]), up(cx[u])
        for core in range(PAIR):
            row = (u * PAIR + core) * ROWS
            cs[row : row + ROWS] = jnp.where(c == core, own, got)[0:ROWS]
    for s in range(2):
        cols = slice(s * GATE.width, (s + 1) * GATE.width)
        zb[z, :, cols] = cs[:, cols].astype(BF)
        for k in range(2):
            zcopy(s, k).start()
    gate = [Gathered(here, GATE, (o0, o1), (gsend, grecv), u, s) for u in range(GATE.units) for s in range(2)]
    down = [Gathered(here, DOWN, (od,), (dsend, drecv), l, s) for l in range(L) for s in range(2)]
    for l in range(L):
        swap_d(l, 1 - c, mine).wait_recv()
    for st in down:
        st.start(0)
    for s in range(2):
        for k in range(2):
            zcopy(s, k).wait_recv()
            zcopy(s, 2 + k).start()
    for st in down:
        st.forward(0)

    for s in range(2):
        cols = slice(s * GATE.width, (s + 1) * GATE.width)
        for k in range(2, 4):
            zcopy(s, k).wait_recv()
        for i in range(RING):
            zm[...] = up(zb[i, :, cols])
            for u in range(GATE.units):
                n = PAIR * ROWS
                zf[u, i * n : i * n + n] = zm[u * n : u * n + n]
        for st in gate[s::2]:
            (o0, o1)[st.u // L][st.u % L, x, y, 0, :, st.whole[0]] = zf[st.u].astype(BF)
            st.start(1)
    for st in down:
        st.end(0)
    both = gate[: L * 2] + down[:2] + gate[L * 2 :] + down[2:]
    for phase in (1, 2):
        for st in both:
            st.forward(phase)
        for st in both:
            st.end(phase)
    for u in range(GATE.units):
        swap_g(u).wait_send()
    for l in range(L):
        swap_d(l, c, theirs).wait_send()
    for s in range(2):
        for k in range(4):
            zcopy(s, k).wait_send()
    for st in both:
        for phase in range(1 if st.cut.gate else 0, PHASES):
            for k in range(4):
                st.copy(phase, k).wait_send()
        for r in range(RING):
            st.across(r).wait_send()
            st.across(r, 1).wait_recv()


def ag(wg, wd):
    block = (RING, RING, 1, ZROWS, FF)
    outs = [pltpu.VMEM((L,) + block, BF)] * 2 + [pltpu.VMEM((L, RING, RING, RING, PAIR, DROWS, D), BF)]
    n, sems = GATE.units, PHASES * 4 + RING
    scratch = [vmem((ZROWS, HG), F32), vmem((n, 16, HG), BF), vmem((RING, ZROWS, HG), BF), vmem((n, ZROWS, GATE.width), F32), vmem((ZROWS, GATE.width), F32)]
    scratch += [dma((n + L,))] * 2 + [dma((2, 4))] * 2 + [dma((n, 2, sems))] * 2 + [dma((L, 2, sems))] * 2
    return call(ag_kernel, outs, [VM] * 2, scratch, "ag", vmem_limit=5 * 2**20, ident=3, out_specs=[VM] * 3)(wg, wd)


def put_kernel(src, dst, sem):
    copies = [pltpu.make_async_copy(src.at[l], dst.at[l], sem.at[l]) for l in range(L)]
    for cp in copies:
        cp.start()
    for cp in copies:
        cp.wait()


def put(w):
    return call(put_kernel, [out(w.shape, BF)], [VM], [dma((L,))], "put", vmem_limit=2**20)(w)[0]


def normed(h):
    wide = up(h)
    scale = lax.rsqrt(jnp.mean(wide**2, -1, keepdims=True) + 1e-6)
    return (wide * scale).astype(BF), scale


def normed_back(h, scale, da):
    wide, da = up(h), up(da)
    mean = jnp.mean(da * wide, -1, keepdims=True)
    return (da * scale - wide * (scale * scale * scale * mean)).astype(BF)


def mm(a, b, across=0):
    return lax.dot_general(a, b, (((1,), (across,)), ((), ())), preferred_element_type=F32)


def gated(gate, u):
    return (jax.nn.silu(gate) * u).astype(BF)


def gated_back(gate, u, dhid):
    sig = jax.nn.sigmoid(gate)
    d = up(dhid)
    return (d * u * (sig * (1 + gate * (1 - sig)))).astype(BF), (d * (gate * sig)).astype(BF)


def device_step(x, dy, wg, wu, wd, *moments):
    x, dy = x[0], dy[0]
    a0, _ = normed(x)
    g0, u0 = mm(a0, wg[0]), mm(a0, wu[0])
    hid0 = gated(g0, u0)
    h1 = x + mm(hid0, wd[0]).astype(BF)
    a1, s1 = normed(h1)
    g1, u1 = mm(a1, wg[1]), mm(a1, wu[1])
    hid1 = gated(g1, u1)
    dg1, du1 = gated_back(g1, u1, mm(dy, wd[1], 1).astype(BF))
    pg1, pu1, pd1 = dw(a1, dg1, du1, hid1, dy)
    da1 = mm(dg1, wg[1], 1).astype(BF) + mm(du1, wu[1], 1).astype(BF)
    dx1 = dy + normed_back(h1, s1, da1)
    dg0, du0 = gated_back(g0, u0, mm(dx1, wd[0], 1).astype(BF))
    pg0, pu0, pd0 = dw(a0, dg0, du0, hid0, dx1)
    gg, gd, norm = rs((pg0, pg1, pu0, pu1), (pd0, pd1))
    moments, ng, nd = adamw(gg, gd, norm, moments, (wg, wu, wd))
    return (*(put(new).reshape(w.shape) for new, w in zip(ag(ng, nd), (wg, wu, wd))), *moments)


def solution(mesh):
    rows, moment, whole = P(("rep", "dp"), None, None), P(None, "dp", None), P(None, None, None)
    return jax.shard_map(
        device_step,
        mesh=mesh,
        in_specs=(rows,) * 2 + (whole,) * 3 + (moment,) * 6,
        out_specs=(P("rep", None, None),) * 3 + (P("rep", "dp", None),) * 6,
        check_vma=False,
    )
```

time: 982 us -> 492 us (0.50)
  blocking collectives: 432 us -> 0 us
  Pallas kernels: 0 us -> 332 us
  waiting for transfers between devices: 221 us -> 0 us
  matrix products: 218 us -> 141 us
  local copies, waits for them, and re-layouts: 51.5 us -> 3.43 us
  other arithmetic: 33.8 us -> 6.37 us
  between operations: 17 us -> 1.42 us
    unnamed x1 -> x0, blocking collectives: 368 us -> none
    pallas_call x0 -> x8, Pallas kernels: none -> 332 us  [the longest x1 120 us: rs(): call(rs_kernel, [out((GATE.units, 16, FF), BF), out((L, DROWS, D), BF), o...]
    reshape x3 -> x0, waiting for transfers between devices: 213 us -> none  [step(): t.reshape(-1, *t.shape[2:])]
    dot_general x15 -> x9, matrix products: 218 us -> 141 us  [mm(): lax.dot_general(a, b, (((1,), (across,)), ((), ())), preferred_element_ty...]
    reduce_sum x1 -> x0, blocking collectives: 64.3 us -> none  [of_a_group(): jnp.sum(g * g)]
    unnamed x63 -> x42, local copies, waits for them, and re-layouts: 47.9 us -> 3.43 us
    unnamed x6 -> x1, other arithmetic: 23.1 us -> 0.01 us
  transfers between devices with their start and end apart: 5 -> 0, of which waited for: 4 -> 0; matrix products, arithmetic and copies ran while one was open for 12% -> 0% of each run, Pallas kernels for 0% -> 0%
where the time goes in v1:
time: 492 us; the launch traced here: 484 us
  Pallas kernels  332 us (67%)
  matrix products  141 us (29%)
  other arithmetic  6.37 us (1%)
    dot_general x9, matrix products, mm(): lax.dot_general(a, b, (((1,), (across,)), ((), ())), preferred_element_ty...  141 us
    pallas_call x1, Pallas kernels, rs(): call(rs_kernel, [out((GATE.units, 16, FF), BF), out((L, DROWS, D), BF), o...  120 us
    pallas_call x1, Pallas kernels, ag(): call(ag_kernel, outs, [VM] * 2, scratch, 'ag', vmem_limit=5 * 2 ** 20, id...  113 us
    pallas_call x2, Pallas kernels, dw(): call(dw_kernel, [out((D, HG), BF)] * 2 + [out((FF, HD), BF)], [HBM] * 5,...  75.9 us
    pallas_call x3, Pallas kernels, put(): call(put_kernel, [out(w.shape, BF)], [VM], [dma((L,))], 'put', vmem_limit...  17.5 us

profile of v1, /device:TPU:1, one launch (start us, length us, event | category | flops | bytes accessed | tf_op | source)
XLA Modules:
  0.0 483.8 jit_solution(2933824842633313697)
XLA Ops:
  0.6 2.3 fusion.41
  3.0 0.0 copy-start.14
  3.0 0.0 copy-start.2
  3.0 14.3 %fusion.22 = f32[1024,3072]{1,0:T(8,128)} fusion(bf16[2,1280,3072]{2,1,0:T(8,128)(2,1)} %refs_6_.1, bf16[1,1024,1280]{2,1,0:T(8,128)(2,1)} %param.11, f32[1024]{0:T(1024)S(1)} %add_rsqrt_fusion.1), kind=kOutput, calls=%fused_computation.34 | convolution fusion | flops 8056995840 | bytes 23072768 | tf_op jit(solution)/shard_map/dot_general | solution.py:634
  17.3 0.0 copy-done.14
  17.3 0.0 copy-done.2
  17.3 18.0 %multiply_convert_fusion.1 = (bf16[1024,3072]{1,0:T(8,128)(2,1)}, f32[1024,3072]{1,0:T(8,128)}) fusion(f32[1024,3072]{1,0:T(8,128)} %fusion.22, bf16[2,1280,3072]{2,1,0:T(8,128)(2,1)} %refs_7_.1, bf16[1,1024,1280]{2,1,0:T(8,128)(2,1)S(1)} %copy-done.2, f32[1024]{0:T(1024)S(1)} %add_rsqrt_fusion.1), kind=kOutput, calls=%fused_computation.13 | convolution fusion | flops 8075870208 | bytes 41947136 | tf_op jit(solution)/shard_map/dot_general | solution.py:634
  35.3 12.9 %fusion.45 = (f32[1024]{0:T(1024)S(1)}, bf16[1024,1280]{1,0:T(8,128)(2,1)S(1)}) fusion(bf16[1024,3072]{1,0:T(8,128)(2,1)} %get-tuple-element.54.hid, bf16[2,3072,1280]{2,1,0:T(8,128)(2,1)} %refs_8_.1, bf16[1,1024,1280]{2,1,0:T(8,128)(2,1)S(1)} %copy-done.2), kind=kOutput, calls=%fused_computation.56 | convolution fusion | flops 8059616256 | bytes 19402752 | tf_op jit(solution)/shard_map/dot_general | solution.py:634
  48.3 0.0 copy-start.12
  48.3 0.0 copy-start.4
  48.3 0.6 copy-done.12
  48.9 0.9 copy-done.4
  49.8 0.0 copy-done.10
  49.8 0.5 fusion.46.a
  50.3 0.0 copy-start.6
  50.3 0.0 slice-start.1
  50.3 0.0 slice-start.2
  50.3 0.0 slice-start.3
  50.3 0.0 copy-start.7
  50.3 15.1 %fusion.10 = f32[1024,3072]{1,0:T(8,128)} fusion(bf16[1024,1280]{1,0:T(8,128)(2,1)S(1)} %fusion.46.a, bf16[2,1280,3072]{2,1,0:T(8,128)(2,1)} %refs_6_.1), kind=kOutput, calls=%fused_computation.22 | convolution fusion | flops 8053063680 | bytes 23068672 | tf_op jit(solution)/shard_map/dot_general | solution.py:634
  65.4 0.0 slice-done.3
  65.4 0.0 copy-done.7
  65.4 10.2 %fusion.35 = bf16[1024,3072]{1,0:T(8,128)(2,1)} fusion(bf16[2,3072,1280]{2,1,0:T(8,128)(2,1)S(1)} %bitcast.86, bf16[1,1024,1280]{2,1,0:T(8,128)(2,1)S(1)} %copy-done.7), kind=kOutput, calls=%fused_computation.50 | convolution fusion | flops 8056209408 | bytes 16777216 | tf_op jit(solution)/shard_map/dot_general | solution.py:634
  75.7 0.0 copy-done.6
  75.7 21.5 %multiply_convert_fusion = (bf16[1024,3072]{1,0:T(8,128)(2,1)}, bf16[1024,3072]{1,0:T(8,128)(2,1)}, bf16[1024,3072]{1,0:T(8,128)(2,1)}) fusion(f32[1024,3072]{1,0:T(8,128)} %fusion.10, bf16[1024,3072]{1,0:T(8,128)(2,1)} %fusion.35, bf16[1024,1280]{1,0:T(8,128)(2,1)S(1)} %fusion.46.a, bf16[2,1280,3072]{2,1,0:T(8,128)(2,1)} %refs_7_.1), kind=kOutput, calls=%fused_computation.10 | convolution fusion | flops 8103395328 | bytes 48234496 | tf_op jit(solution)/shard_map/dot_general | solution.py:634
  97.2 38.6 %dw.3 = (bf16[1280,1536]{1,0:T(8,128)(2,1)}, bf16[1280,1536]{1,0:T(8,128)(2,1)}, bf16[3072,640]{1,0:T(8,128)(2,1)}) custom-call(bf16[1024,1280]{1,0:T(8,128)(2,1)} %copy-done.6, bf16[1024,3072]{1,0:T(8,128)(2,1)} %get-tuple-element.50.dg, bf16[1024,3072]{1,0:T(8,128)(2,1)} %get-tuple-element.51.du, bf16[1024,3072]{1,0:T(8,128)(2,1)} %get-tuple-element.49.hid, ...), custom_call_target="tpu_custom_call" | custom-call | flops 24159191040 | bytes 25165824 | tf_op jit(solution)/shard_map/dw/pallas_call | solution.py:175
  135.8 13.9 %fusion.51 = bf16[1024,1280]{1,0:T(8,128)(2,1)} fusion(bf16[1024,3072]{1,0:T(8,128)(2,1)} %get-tuple-element.51.du, bf16[2,1280,3072]{2,1,0:T(8,128)(2,1)} %refs_7_.1), kind=kOutput, calls=%fused_computation.61 | convolution fusion | flops 8054374400 | bytes 16777216 | tf_op jit(solution)/shard_map/dot_general | solution.py:634
  149.7 0.0 copy-done.5
  149.7 0.0 copy-start.8
  149.8 0.0 copy-start.11
  149.8 12.9 %fusion.47 = (f32[1024]{0:T(1024)S(1)}, bf16[1024,1280]{1,0:T(8,128)(2,1)S(1)}) fusion(bf16[1024,1280]{1,0:T(8,128)(2,1)S(1)} %copy-done.5, bf16[1024,1280]{1,0:T(8,128)(2,1)} %fusion.51, bf16[1024,3072]{1,0:T(8,128)(2,1)S(1)} %copy-done.16, bf16[2,1280,3072]{2,1,0:T(8,128)(2,1)} %refs_6_.1), kind=kOutput, calls=%fused_computation.58 | convolution fusion | flops 8060926976 | bytes 22024192 | tf_op jit(solution)/shard_map/dot_general | solution.py:634
  162.7 1.6 fusion.64.dy
  164.3 0.0 copy-start.9
  164.3 0.0 copy-start.3
  164.3 0.0 copy-start.15
  164.3 21.8 %fusion.5 = (bf16[1024,3072]{1,0:T(8,128)(2,1)}, bf16[1024,3072]{1,0:T(8,128)(2,1)}) fusion(f32[1024,3072]{1,0:T(8,128)} %fusion.22, f32[1024,3072]{1,0:T(8,128)} %get-tuple-element.55, bf16[1024,1280]{1,0:T(8,128)(2,1)S(1)} %fusion.64.dy, bf16[2,3072,1280]{2,1,0:T(8,128)(2,1)} %refs_8_.1), kind=kOutput, calls=%fused_computation.9 | convolution fusion | flops 8100249600 | bytes 48234496 | tf_op jit(solution)/shard_map/dot_general | solution.py:634
  186.1 0.0 copy-done.9
  186.2 2.0 fusion.42.a
  188.1 37.3 %dw.2 = (bf16[1280,1536]{1,0:T(8,128)(2,1)}, bf16[1280,1536]{1,0:T(8,128)(2,1)}, bf16[3072,640]{1,0:T(8,128)(2,1)}) custom-call(bf16[1024,1280]{1,0:T(8,128)(2,1)} %fusion.42.a, bf16[1024,3072]{1,0:T(8,128)(2,1)} %get-tuple-element.53.dg, bf16[1024,3072]{1,0:T(8,128)(2,1)} %get-tuple-element.52.du, bf16[1024,3072]{1,0:T(8,128)(2,1)} %get-tuple-element.54.hid, ...), custom_call_target="tpu_custom_call" | custom-call | flops 24159191040 | bytes 25165824 | tf_op jit(solution)/shard_map/dw/pallas_call | solution.py:175
  225.4 120.3 %rs.1 = (bf16[4,16,3072]{2,1,0:T(8,128)(2,1)}, bf16[2,24,1280]{2,1,0:T(8,128)(2,1)}, f32[8,128]{1,0:T(8,128)}) custom-call(bf16[4,4,1,80,1536]{4,3,2,1,0:T(8,128)(2,1)} %bitcast.93, bf16[4,4,1,80,1536]{4,3,2,1,0:T(8,128)(2,1)} %bitcast.90, bf16[4,4,1,80,1536]{4,3,2,1,0:T(8,128)(2,1)} %bitcast.94, bf16[4,4,1,80,1536]{4,3,2,1,0:T(8,128)(2,1)} %bitcast.91, ...), custom_call_target="tpu_custom_call" | custom-call | tf_op jit(solution)/shard_map/rs/pallas_call | solution.py:418
  345.7 5.2 %adamw.1 = (f32[10,2,3072]{2,1,0:T(2,128)}, f32[10,2,3072]{2,1,0:T(2,128)}, f32[2,24,1280]{2,1,0:T(8,128)}, f32[10,2,3072]{2,1,0:T(2,128)}, f32[10,2,3072]{2,1,0...) custom-call(bf16[4,16,3072]{2,1,0:T(8,128)(2,1)} %get-tuple-element.35.gg, ...), custom_call_target="tpu_custom_call" | custom-call | tf_op jit(solution)/shard_map/adamw/pallas_call | solution.py:464
  350.9 0.0 copy-start
  350.9 1.0 copy-done
  351.9 0.9 copy-done.1
  352.8 113.0 %ag.1 = (bf16[2,4,4,1,80,3072]{5,4,3,2,1,0:T(8,128)(2,1)S(1)}, bf16[2,4,4,1,80,3072]{5,4,3,2,1,0:T(8,128)(2,1)S(1)}, bf16[2,4,4,4,2,24,1280]{6,5,4,3,2,1,0:T(8,128)(2,1)S(1)}) custom-call(bf16[4,16,3072]{2,1,0:T(8,128)(2,1)S(1)} %copy-done, bf16[2,24,1280]{2,1,0:T(8,128)(2,1)S(1)} %copy-done.1), custom_call_target="tpu_custom_call" | custom-call | tf_op jit(solution)/shard_map/ag/pallas_call | solution.py:606
  465.8 5.8 %put.3 = bf16[2,4,4,1,80,3072]{5,4,3,2,1,0:T(8,128)(2,1)} custom-call(bf16[2,4,4,1,80,3072]{5,4,3,2,1,0:T(8,128)(2,1)S(1)} %get-tuple-element.40.src), custom_call_target="tpu_custom_call" | custom-call | tf_op jit(solution)/shard_map/put/pallas_call | solution.py:618
  471.7 5.8 %put.4 = bf16[2,4,4,1,80,3072]{5,4,3,2,1,0:T(8,128)(2,1)} custom-call(bf16[2,4,4,1,80,3072]{5,4,3,2,1,0:T(8,128)(2,1)S(1)} %get-tuple-element.41.src), custom_call_target="tpu_custom_call" | custom-call | tf_op jit(solution)/shard_map/put/pallas_call | solution.py:618
  477.5 5.8 %put.5 = bf16[2,4,4,4,2,24,1280]{6,5,4,3,2,1,0:T(8,128)(2,1)} custom-call(bf16[2,4,4,4,2,24,1280]{6,5,4,3,2,1,0:T(8,128)(2,1)S(1)} %get-tuple-element.42.src), custom_call_target="tpu_custom_call" | custom-call | tf_op jit(solution)/shard_map/put/pallas_call | solution.py:618
  (19 shorter events, 0.1 us)
Async XLA Ops:
  3.0 14.4 %copy-start.14 = (f32[1024]{0:T(1024)}, f32[1024]{0:T(1024)S(1)}, u32[]{:S(2)}) copy-start(f32[1024]{0:T(1024)S(1)} %add_rsqrt_fusion.1) | copy-start | bytes 12292
  3.0 14.4 %copy-start.2 = (bf16[1,1024,1280]{2,1,0:T(8,128)(2,1)S(1)}, bf16[1,1024,1280]{2,1,0:T(8,128)(2,1)}, u32[]{:S(2)}) copy-start(bf16[1,1024,1280]{2,1,0:T(8,128)(2,1)} %param.11) | copy-start | bytes 7864324
  48.3 0.6 copy-start.12
  48.3 1.5 copy-start.4
  48.9 0.9 copy-start.10
  49.8 15.7 %slice-start = ((s8[15728640]{0:T(1024)(128)(4,1)}), s8[4194304]{0:T(1024)(128)(4,1)S(1)}, s32[]{:S(2)}) async-start(s8[15728640]{0:T(1024)(128)(4,1)} %bitcast.85), calls=%async_computation | async-start | bytes 8388608
  50.3 25.4 %copy-start.6 = (bf16[1024,1280]{1,0:T(8,128)(2,1)}, bf16[1024,1280]{1,0:T(8,128)(2,1)S(1)}, u32[]{:S(2)}) copy-start(bf16[1024,1280]{1,0:T(8,128)(2,1)S(1)} %fusion.46.a) | copy-start | bytes 7864324
  50.3 15.1 %slice-start.1 = ((s8[15728640]{0:T(1024)(128)(4,1)}), s8[4194304]{0:T(1024)(128)(4,1)S(1)}, s32[]{:S(2)}) async-start(s8[15728640]{0:T(1024)(128)(4,1)} %bitcast.85), calls=%async_computation.1 | async-start | bytes 8388608
  50.3 15.1 %slice-start.2 = ((s8[15728640]{0:T(1024)(128)(4,1)}), s8[4194304]{0:T(1024)(128)(4,1)S(1)}, s32[]{:S(2)}) async-start(s8[15728640]{0:T(1024)(128)(4,1)} %bitcast.85), calls=%async_computation.2 | async-start | bytes 8388608
  50.3 15.1 %slice-start.3 = ((s8[15728640]{0:T(1024)(128)(4,1)}), s8[3145728]{0:T(1024)(128)(4,1)S(1)}, s32[]{:S(2)}) async-start(s8[15728640]{0:T(1024)(128)(4,1)} %bitcast.85), calls=%async_computation.3 | async-start | bytes 6291456
  50.3 15.1 %copy-start.7 = (bf16[1,1024,1280]{2,1,0:T(8,128)(2,1)S(1)}, bf16[1,1024,1280]{2,1,0:T(8,128)(2,1)}, u32[]{:S(2)}) copy-start(bf16[1,1024,1280]{2,1,0:T(8,128)(2,1)} %param.12) | copy-start | bytes 7864324
  135.8 14.0 %copy-start.5 = (bf16[1024,1280]{1,0:T(8,128)(2,1)S(1)}, bf16[1024,1280]{1,0:T(8,128)(2,1)}, u32[]{:S(2)}) copy-start(bf16[1024,1280]{1,0:T(8,128)(2,1)} %copy-done.4) | copy-start | bytes 7864324
  135.8 13.9 %copy-start.16 = (bf16[1024,3072]{1,0:T(8,128)(2,1)S(1)}, bf16[1024,3072]{1,0:T(8,128)(2,1)}, u32[]{:S(2)}) copy-start(bf16[1024,3072]{1,0:T(8,128)(2,1)} %get-tuple-element.50.dg) | copy-start | bytes 18874372
  149.7 12.9 %copy-start.13 = (f32[1024]{0:T(1024)S(1)}, f32[1024]{0:T(1024)}, u32[]{:S(2)}) copy-start(f32[1024]{0:T(1024)} %copy-done.12) | copy-start | bytes 12292
  149.7 12.9 %copy-start.8 = (bf16[1,1024,1280]{2,1,0:T(8,128)(2,1)S(1)}, bf16[1,1024,1280]{2,1,0:T(8,128)(2,1)}, u32[]{:S(2)}) copy-start(bf16[1,1024,1280]{2,1,0:T(8,128)(2,1)} %param.12) | copy-start | bytes 7864324
  149.8 12.9 %copy-start.11 = (f32[1024]{0:T(1024)S(1)}, f32[1024]{0:T(1024)}, u32[]{:S(2)}) copy-start(f32[1024]{0:T(1024)} %copy-done.10) | copy-start | bytes 12292
  164.3 21.9 %copy-start.9 = (bf16[1024,1280]{1,0:T(8,128)(2,1)}, bf16[1024,1280]{1,0:T(8,128)(2,1)S(1)}, u32[]{:S(2)}) copy-start(bf16[1024,1280]{1,0:T(8,128)(2,1)S(1)} %fusion.64.dy) | copy-start | bytes 7864324
  164.3 21.9 %copy-start.3 = (bf16[1,1024,1280]{2,1,0:T(8,128)(2,1)S(1)}, bf16[1,1024,1280]{2,1,0:T(8,128)(2,1)}, u32[]{:S(2)}) copy-start(bf16[1,1024,1280]{2,1,0:T(8,128)(2,1)} %param.11) | copy-start | bytes 7864324
  164.3 21.9 %copy-start.15 = (f32[1024]{0:T(1024)S(1)}, f32[1024]{0:T(1024)}, u32[]{:S(2)}) copy-start(f32[1024]{0:T(1024)} %copy-done.14) | copy-start | bytes 12292
  350.9 1.0 copy-start
  351.9 0.9 copy-start.1

commit v2 on v1

v2 whole, which is shorter than its diff:
```python
import functools

import jax
import jax.numpy as jnp
from jax import lax
from jax.experimental import pallas as pl
from jax.experimental.pallas import tpu as pltpu
from jax.sharding import PartitionSpec as P

BF, F32 = jnp.bfloat16, jnp.float32
T, D, FF = 1024, 1280, 3072
L, RING, PAIR = 2, 4, 2
X, Y, Z, CORE = range(4)
HG, HD = FF // PAIR, D // PAIR
ROWS, DROWS = D // (RING**3 * PAIR), FF // (RING**3 * PAIR)
ZROWS = PAIR * RING * ROWS
NT = 256
WIDE = 512
PAD = 24
MOST = 67043328
HBM, VM = pl.BlockSpec(memory_space=pltpu.HBM), pl.BlockSpec(memory_space=pltpu.VMEM)
dma, vmem = pltpu.SemaphoreType.DMA, pltpu.VMEM
out = jax.ShapeDtypeStruct
ALL, BOTH = slice(None), range(2)
PAIR_SEM, PAIRS_SEM = dma((2,)), dma((2, 2))


class Place:
    def __init__(self):
        i = lax.axis_index("dp")
        chip, core = lax.div(i, PAIR), lax.rem(i, PAIR)
        self.at = [[lax.div(chip, RING**2)], [lax.rem(lax.div(chip, RING), RING)], [lax.rem(chip, RING)], [core, 1 - core]]
        for steps in self.at[:CORE]:
            steps += [lax.rem(steps[0] + r, RING) for r in range(1, RING)]
        self.peers = {}

    def moved(self, dim, by=1):
        by %= len(self.at[dim])
        if (dim, by) not in self.peers:
            x, y, z, core = (steps[by if d == dim else 0] for d, steps in enumerate(self.at))
            self.peers[dim, by] = {"dp": ((x * RING + y) * RING + z) * PAIR + core}
        return self.peers[dim, by]


def meet(peers):
    barrier = pltpu.get_barrier_semaphore()
    for peer in peers:
        pl.semaphore_signal(barrier, inc=1, device_id=peer)
    pl.semaphore_wait(barrier, len(peers))


def remote(src, dst, send, recv, peer):
    return pltpu.make_async_remote_copy(src, dst, send, recv, device_id=peer)


def up(v):
    return v.astype(F32)


def call(kernel, outs, ins, scratch, name, vmem_limit=MOST, ident=None, out_specs=None, **more):
    return pl.pallas_call(
        kernel,
        out_shape=outs,
        in_specs=ins,
        out_specs=out_specs or [HBM] * len(outs),
        scratch_shapes=scratch,
        compiler_params=pltpu.CompilerParams(collective_id=ident, has_side_effects=ident is not None, vmem_limit_bytes=vmem_limit),
        name=name,
        **more,
    )


def odd(i):
    return lax.rem(i, 2)


def tiled(n, body, hooks=(), base=0):
    def one(i, _):
        body(i)
        for k, hook in hooks:
            pl.when(base + i == k)(hook)
        return _

    lax.fori_loop(0, n, one, 0)


class Loaded:
    def __init__(self, n, src, buf, sem):
        self.n, self.src, self.buf, self.sem = n, src, buf, sem

    def copy(self, i):
        slot = odd(i)
        return pltpu.make_async_copy(self.src(i), self.buf.at[slot], self.sem.at[slot])

    def start(self):
        self.copy(jnp.int32(0)).start()

    def ready(self, i):
        pl.when(i + 1 < self.n)(lambda: self.copy(i + 1).start())
        self.copy(i).wait()

    def take(self, i):
        self.ready(i)
        return odd(i)


def mm(a, b, across=0):
    return lax.dot_general(a, b, (((1,), (across,)), ((), ())), preferred_element_type=F32)


def tn(a, b):
    return lax.dot_general(a, b, (((0,), (0,)), ((), ())), preferred_element_type=F32).astype(BF)


def at(i, n, base=0):
    return pl.ds(pl.multiple_of(base + i * n, 128), n)


def fetch(pairs, sem):
    copies = [pltpu.make_async_copy(src, dst, sem.at[i]) for i, (src, dst) in enumerate(pairs)]
    for cp in copies:
        cp.start()
    return copies


class Cut:
    def __init__(self, gate):
        self.gate = gate
        self.width = HG // 2 if gate else HD
        self.n, self.rows = (1, ZROWS) if gate else (RING, DROWS)

    def dims(self, s):
        return (s, 1 - s, Z) if self.gate else (Z, s, 1 - s)

    def part(self, s, h, base=0):
        first = 384 if self.gate or s == 0 else 256
        return pl.ds(base + first, self.width - first) if h else pl.ds(base, first)

    def index(self, here, s, dim, r, done, cols):
        at = [here.at[d][r % RING] if d == dim else ALL if d in done else here.at[d][0] for d in (X, Y, Z)]
        return (at[X], at[Y]) + ((ALL,) if self.gate else (at[Z], s)) + (ALL, cols)


GATE, DOWN = Cut(True), Cut(False)


def ahead(k):
    return 1 if k in (0, 3, 4) else -1


PART = T // 4


def in_pairs(body):
    def both(i):
        for k in BOTH:
            body(at(2 * i + k, PART))

    tiled(T // (2 * PART), both)


def normed(src, dst):
    def rows(i):
        r = at(i, PART)
        wide = up(src[r])
        dst[r] = (wide * lax.rsqrt(jnp.mean(wide**2, -1, keepdims=True) + 1e-6)).astype(BF)

    tiled(T // PART, rows)


def gated(gate, u):
    sig = jax.nn.sigmoid(gate)
    silu = gate * sig
    return (silu * u).astype(BF), u * (sig * (1 + gate * (1 - sig))), silu


class Stored:
    def __init__(self, dst, buf, sem):
        self.dst, self.buf, self.sem = dst, buf, sem

    def copy(self, i):
        slot = odd(i)
        return pltpu.make_async_copy(self.buf.at[slot], self.dst(i), self.sem.at[slot])

    def free(self, i):
        pl.when(i >= 2)(lambda: self.copy(i - 2).wait())

    def end(self, n):
        for i in (n - 2, n - 1):
            self.copy(jnp.int32(i)).wait()


HALVES = vmem((2, 2, D, WIDE), BF)
STATES = vmem((T, D), BF)


def forward_kernel(x, dy, wg, wu, wd, oa0, ohid0, ofg, ofu, oh1, oa1, ohid1, od1, vx, va, vhid, vdy, sem, osem, hsem):
    n = FF // WIDE
    x_here, dy_here = fetch([(x, vx), (dy, vdy)], sem)
    wide = lambda ref, l: lambda i: ref.at[l, :, at(i, WIDE)]

    def put(i):
        return pltpu.make_async_copy(vhid.at[:, at(i, WIDE)], ohid0.at[:, at(i, WIDE)], hsem.at[i])

    def first(vw, wsem, vo, vsem):
        tiles = [Loaded(n, wide(w, 0), vw.at[k], wsem.at[k]) for k, w in enumerate((wg, wu))]
        outs = [Stored(lambda i, o=o: o.at[:, at(i, WIDE)], vo.at[k], vsem.at[k]) for k, o in enumerate((ofg, ofu))]
        for t in tiles:
            t.start()
        x_here.wait()
        normed(vx, va)
        a_out, = fetch([(va, oa0)], osem)

        def body(i):
            slot, _ = [t.take(i) for t in tiles]
            for o in outs:
                o.free(i)

            def rows(r):
                vhid[r, at(i, WIDE)], *factors = gated(*(mm(va[r], vw[k, slot]) for k in BOTH))
                for k in BOTH:
                    vo[k, slot, r] = factors[k]

            in_pairs(rows)
            put(i).start()
            for o in outs:
                o.copy(i).start()

        tiled(n, body)
        for o in outs:
            o.end(n)
        a_out.wait()

    pl.run_scoped(first, HALVES, PAIRS_SEM, vmem((2, 2, T, WIDE), F32), PAIRS_SEM)

    def second(vw, wsem):
        tiles = Loaded(D // NT, lambda i: wd.at[0, :, at(i, NT)], vw, wsem)
        tiles.start()

        def body(i):
            slot, cols = tiles.take(i), at(i, NT)

            def rows(r):
                vx[r, cols] = (up(vx[r, cols]) + up(mm(vhid[r], vw[slot]).astype(BF))).astype(BF)

            in_pairs(rows)

        tiled(D // NT, body)

    pl.run_scoped(second, vmem((2, FF, NT), BF), PAIR_SEM)
    for i in range(n):
        put(i).wait()

    def third(vw, wsem, vd, dsem, vo, vsem):
        tiles = [Loaded(n, wide(w, 1), vw.at[k], wsem.at[k]) for k, w in enumerate((wg, wu))]
        tiles.append(Loaded(n, lambda i: wd.at[1, at(i, WIDE), :], vd, dsem))
        outs = [Stored(lambda i, o=o: o.at[:, at(i, WIDE)], vo.at[k], vsem.at[k]) for k, o in enumerate((od1.at[0], od1.at[1], ohid1))]
        for t in tiles:
            t.start()
        normed(vx, va)
        kept = fetch([(vx, oh1), (va, oa1)], osem)
        dy_here.wait()

        def body(i):
            slot, *_ = [t.take(i) for t in tiles]
            for o in outs:
                o.free(i)

            def rows(r):
                hid, *factors = gated(*(mm(va[r], vw[k, slot]) for k in BOTH))
                dhid = up(mm(vdy[r], vd[slot], 1).astype(BF))
                vo[2, slot, r] = hid
                for k in BOTH:
                    vo[k, slot, r] = (dhid * factors[k]).astype(BF)

            in_pairs(rows)
            for o in outs:
                o.copy(i).start()

        tiled(n, body)
        for o in outs:
            o.end(n)
        for cp in kept:
            cp.wait()

    pl.run_scoped(third, HALVES, PAIRS_SEM, vmem((2, WIDE, D), BF), PAIR_SEM, vmem((3, 2, T, WIDE), BF), dma((3, 2)))


def forward(x, dy, wg, wu, wd):
    states, hidden = out((T, D), BF), out((T, FF), BF)
    outs = [states, hidden, out((T, FF), F32), out((T, FF), F32), states, states, hidden, out((2, T, FF), BF)]
    scratch = [STATES] * 2 + [vmem((T, FF), BF), STATES, PAIR_SEM, PAIR_SEM, dma((FF // WIDE,))]
    return call(forward_kernel, outs, [HBM] * 5, scratch, "forward")(x, dy, wg, wu, wd)


SUM, OWN, GOT = range(3)
TILES = 6
TILE = FF // TILES
DOWN_SCRATCH = [vmem((TILES, TILE, HD), BF)] + [dma((TILES,))] * 2 + [dma((GOT + 1, TILES))]
HIDDEN = [vmem((2, T, TILE), BF), PAIR_SEM, vmem((TILES, PAIR, TILE, HD), BF)]
BLOCKS = (RING, RING, 1, ZROWS)
GATE_SCRATCH = [vmem((2, 2) + BLOCKS + (GATE.width,), BF)] * 3 + [PAIRS_SEM] * 2
GATE_SUMS, DOWN_SUMS = out((GOT + 1, 2) + BLOCKS + (HG,), BF), out((GOT + 1, FF, HD), BF)


class DownProduct:
    def __init__(self, here, hid, hbuf, hsem, halves, got, send, recv, outsem):
        self.here, self.halves, self.got, self.send, self.recv, self.outsem = here, halves, got, send, recv, outsem
        self.hidden = Loaded(TILES, lambda i: hid.at[:, at(i, TILE)], hbuf, hsem)
        self.hidden.start()

    def swap(self, i):
        _, theirs = self.here.at[CORE]
        return remote(self.halves.at[i, theirs], self.got.at[i], self.send.at[i], self.recv.at[i], self.here.moved(CORE))

    def put(self, od, i):
        mine, theirs = self.here.at[CORE]
        srcs = self.halves.at[i, theirs], self.halves.at[i, mine], self.got.at[i]
        return [pltpu.make_async_copy(src, od.at[k, at(i, TILE), :], self.outsem.at[k, i]) for k, src in enumerate(srcs)]

    def run(self, dy, od, hooks=()):
        mine, theirs = self.here.at[CORE]

        def add(i):
            self.swap(i).wait()
            self.halves[i, theirs] = (up(self.got[i]) + up(self.halves[i, mine])).astype(BF)
            for cp in self.put(od, i):
                cp.start()

        def body(i):
            full = tn(self.hidden.buf[self.hidden.take(i)], dy[...])
            for half in BOTH:
                self.halves[i, half] = full[:, half * HD : (half + 1) * HD]
            self.swap(i).start()
            pl.when(i > 0)(lambda: add(i - 1))

        tiled(TILES, body, hooks)
        add(TILES - 1)
        for i in range(TILES):
            for cp in self.put(od, i):
                cp.wait()


class GateProducts:
    def __init__(self, here, d, buf, sem, total, own, got, send, recv):
        self.here, self.sems = here, (send, recv)
        self.terms = total, own, got

        def src(i):
            t, (mine, theirs) = lax.rem(i, 4), here.at[CORE]
            return d.at[lax.div(i, 4), :, at(odd(i), GATE.width, jnp.where(t < 2, theirs, mine) * HG)]

        self.tiles = Loaded(8, src, buf, sem)
        self.tiles.start()

    def swap(self, w, t):
        send, recv = self.sems
        return remote(self.terms[SUM].at[w, t], self.terms[GOT].at[w, t], send.at[w, t], recv.at[w, t], self.here.moved(CORE))

    def put(self, og, sem, w, t):
        return [pltpu.make_async_copy(v.at[w, t], og.at[k, w, :, :, :, :, at(t, GATE.width)], sem.at[k, w, t]) for k, v in enumerate(self.terms)]

    def run(self, a, hooks=(), after=lambda w, t: None):
        total, own, got = self.terms

        def product(i):
            return tn(a[...], self.tiles.buf[self.tiles.take(i)]).reshape(BLOCKS + (GATE.width,))

        def matrix(w, _):
            def theirs(t):
                total[w, t] = product(4 * w + t)
                self.swap(w, t).start()

            def mine(t):
                own[w, t] = product(4 * w + 2 + t)
                self.swap(w, t).wait()
                total[w, t] = (up(got[w, t]) + up(own[w, t])).astype(BF)
                after(w, t)

            tiled(2, theirs, hooks, 4 * w)
            tiled(2, mine, hooks, 4 * w + 2)
            return _

        lax.fori_loop(0, 2, matrix, 0)


COLUMNS = [vmem((2, T, GATE.width), BF), PAIR_SEM]


def dw_kernel(a, d, hid, dy, og, od, va, vy, sem, gout, *refs):
    here = Place()
    n = len(HIDDEN + DOWN_SCRATCH)
    down = DownProduct(here, hid, *refs[:n])
    dy_here, a_here = fetch([(dy, vy), (a, va)], sem)
    gates = GateProducts(here, d, *refs[n:])
    meet([here.moved(CORE)])

    def put(w, t):
        for cp in gates.put(og, gout, w, t):
            cp.start()

    dy_here.wait()
    down.run(vy, od)
    a_here.wait()
    gates.run(va, after=put)
    for w in BOTH:
        for t in BOTH:
            for cp in gates.put(og, gout, w, t):
                cp.wait()


def dw(a, d, hid, dy):
    scratch = [STATES] * 2 + [PAIR_SEM, dma((GOT + 1, 2, 2))] + HIDDEN + DOWN_SCRATCH + COLUMNS + GATE_SCRATCH
    return call(dw_kernel, [GATE_SUMS, DOWN_SUMS], [HBM] * 4, scratch, "dw", ident=1)(a, d, hid, dy)


PHASES, COPIES = 3, 6
NAMES = ("r1", "o1", "k2", "r2", "t3", "k3", "r3", "send", "recv", "own")


class Summed:
    def __init__(self, here, cut, src, b, u, s):
        self.here, self.cut, self.src, self.us, self.s, self.dims = here, cut, src, (u, s), s, cut.dims(s)
        self.got, self.kept = [b[k] for k in ("r1", "r2", "r3")], [b[k] for k in ("o1", "k2", "k3")]
        self.t3, self.sems, self.direct = b["t3"], (b["send"], b["recv"], b["own"]), isinstance(src, tuple)

    def block(self, phase, r, cols=ALL, first=()):
        dim = self.dims[phase]
        i = self.here.at[dim][r % RING]
        if phase == 2:
            return self.us + first + (i, ALL, cols)
        second = phase == 1 and not self.cut.gate and self.s
        return self.us + first + ((ALL, i) if second else (i, ALL)) + (ALL, cols)

    def first(self, kind, r, h):
        if self.direct:
            ref, lead, base = self.src[kind], self.us, 0
        else:
            ref, lead, base = self.src, (kind,) + (self.us[:1] if self.cut.gate else ()), self.s * self.cut.width if self.cut.gate else 0
        return ref.at[lead + self.cut.index(self.here, self.s, self.dims[0], r, self.dims, self.cut.part(self.s, h, base))]

    def term(self, n, cols=ALL, r=0):
        if self.direct:
            i = self.here.at[self.dims[0]][r % RING]
            at_, terms = [self.us + ((n, i) if self.s else (i, n)) + (ALL, ALL, cols)] * 2, self.src[OWN:]
        else:
            at_, terms = [self.us + (k, n, ALL, ALL, cols) for k in BOTH], [self.kept[0]] * 2
        return sum(up(ref[i]) for ref, i in zip(terms, at_))

    def at(self, phase, kind, cols=ALL):
        return self.us + (kind,) + (ALL,) * (PHASES - phase) + (cols,)

    def copy(self, phase, k):
        kind, h = k // 2, k % 2
        cols = self.cut.part(self.s, h)
        got = self.got[phase]
        r = (2, -ahead(h), 0)[kind]
        if kind == 2:
            src = got.at[self.at(phase, 0, cols)]
        elif phase == 0:
            src = self.first(SUM, r, h)
        elif phase == 1:
            src = self.got[0].at[self.block(1, r, cols, (2,))]
        else:
            src = self.t3.at[self.block(2, r, cols)]
        send, recv, _ = self.sems
        i = self.us + (phase * COPIES + k,)
        return remote(src, got.at[self.at(phase, kind, cols)], send.at[i], recv.at[i], self.here.moved(self.dims[phase], ahead(k)))

    def own(self, k):
        kind, h = k // 2, k % 2
        cols, copies = self.cut.part(self.s, h), []
        for term in () if self.direct else BOTH:
            dst = self.kept[0].at[self.us + (term,) + (ALL,) * PHASES + (cols,)]
            copies.append(pltpu.make_async_copy(self.first(OWN + term, 0 if kind else ahead(h), h), dst, self.sems[2].at[self.us + (k, term)]))
        return copies

    def start(self, part):
        for h in BOTH:
            self.copy(0, 2 * part + h).start()
            for cp in [] if part else self.own(h):
                cp.start()

    def arrive(self, ks):
        for k in ks:
            for cp in self.own(k):
                cp.wait()

    def pass_on(self, phase):
        got, kept = self.got[phase], self.kept[phase]
        for h in BOTH:
            self.copy(phase, h).wait_recv()
            cols = self.cut.part(self.s, h)
            if phase:
                i = self.at(phase, 0, cols)
                got[i] = (up(got[i]) + kept[self.block(phase, ahead(h), cols)]).astype(BF)
            else:
                self.arrive([h])

                def add(n):
                    i = self.us + (0, n, ALL, ALL, cols)
                    got[i] = (up(got[i]) + self.term(n, cols, ahead(h))).astype(BF)

                tiled(RING, add)
            self.copy(phase, 4 + h).start()
        for h in () if phase else BOTH:
            for cp in self.own(2 + h):
                cp.start()

    def finish(self, phase):
        for k in range(2, COPIES):
            self.copy(phase, k).wait_recv()
        got, kept = self.got[phase], self.kept[phase]
        if phase:
            return kept[self.block(phase, 0)] + up(got[self.us + (2,)]) + up(got[self.us + (1,)])
        self.arrive((2, 3))

        def add(n):
            total = self.term(n) + up(got[self.us + (2, n)]) + up(got[self.us + (1, n)])
            self.kept[1][self.us + (n,)] = total
            got[self.us + (2, n)] = total.astype(BF)

        tiled(RING, add)

    def starts(self, phase):
        for k in range(4):
            self.copy(phase, k).start()


class Sums:
    def __init__(self, here, og, od, refs):
        self.here = here
        n = len(NAMES)
        bufs = [dict(zip(NAMES, refs[i : i + n])) for i in (0, n)]
        self.f3, self.f4, self.ce, self.cr, self.co, self.fd, self.dr, self.csend, self.crecv, self.putsem = refs[2 * n :]
        self.gate, self.upper = ([Summed(here, GATE, og, bufs[0], u, s) for s in BOTH] for u in BOTH)
        self.down = [Summed(here, DOWN, od, bufs[1], 0, s) for s in BOTH]
        self.puts = []
        self.f3[ZROWS : ZROWS + 8] = jnp.zeros((8, GATE.width), F32)
        self.f4[PAD : PAD + 8] = jnp.zeros((8, HG), F32)

    def begin(self, streams):
        for part in BOTH:
            for st in streams:
                st.start(part)

    def second(self, st):
        total = st.finish(1)
        if st.cut.gate:
            self.f3[0:ZROWS] = total[0]
            for i in range(RING):
                rows = self.f3[i * PAIR * ROWS : i * PAIR * ROWS + PAD]
                st.kept[2][st.us + (i,)] = rows
                st.t3[st.us + (i,)] = rows.astype(BF)
        else:
            st.kept[2][st.us] = total
            st.t3[st.us] = total.astype(BF)

    def step(self, n, *streams):
        for st in streams:
            if n % 2 == 0:
                st.pass_on(n // 2)
            else:
                if n == 1:
                    st.finish(0)
                else:
                    self.second(st)
                st.starts(n // 2 + 1)

    def swap(self, u):
        src, dst = (self.fd.at[self.here.at[CORE][1]], self.dr) if u == 2 else (self.ce.at[u], self.cr.at[u])
        return remote(src, dst, self.csend.at[u], self.crecv.at[u], self.here.moved(CORE))

    def last(self, u):
        if u == 2:
            for st in self.down:
                self.fd[st.s] = st.finish(2).astype(BF)
            parts = [up(self.fd[s]) for s in BOTH]
        else:
            for st in self.upper if u else self.gate:
                self.f4[0:PAD, st.s * GATE.width : (st.s + 1) * GATE.width] = st.finish(2)
            low, high = self.f4[0:16], self.f4[ROWS : ROWS + 16]
            first = self.here.at[CORE][0] == 0
            self.co[u] = jnp.where(first, low, high).astype(BF)
            self.ce[u] = jnp.where(first, high, low).astype(BF)
            valid = lax.broadcasted_iota(jnp.int32, (PAD, HG), 0) < PAIR * ROWS
            parts = [jnp.where(valid, up(self.f4[0:PAD].astype(BF)), 0.0)]
        self.swap(u).start()
        return sum(squares(v) for v in parts)

    def put(self, src, dst):
        self.puts.append(pltpu.make_async_copy(src, dst, self.putsem.at[len(self.puts)]))
        self.puts[-1].start()

    def results(self, gg, gd):
        mine, theirs = self.here.at[CORE]
        for u in range(3):
            n, dst = (HD, gd) if u == 2 else (HG, gg.at[u])
            self.put(self.fd.at[mine] if u == 2 else self.co.at[u], dst.at[:, at(mine, n)])
            self.swap(u).wait()
            self.put(self.dr if u == 2 else self.cr.at[u], dst.at[:, at(theirs, n)])

    def drain(self):
        for st in self.down + self.gate + self.upper:
            for k in range(PHASES * COPIES):
                st.copy(k // COPIES, k % COPIES).wait_send()
        for cp in self.puts:
            cp.wait()


def squares(v):
    v = v * v
    rows = sum(v[i : i + 8] for i in range(0, v.shape[0], 8))
    return sum(rows[:, i : i + 128] for i in range(0, v.shape[1], 128))


LANES = vmem((8, 128), F32)


def sums_scratch(direct):
    scratch = []
    for cut, units in ((GATE, 2), (DOWN, 1)):
        us, block, width = (units, 2), (cut.n, cut.rows, cut.width), cut.width
        terms = LANES if direct and cut.gate else vmem(us + (2, RING) + block, BF)
        scratch += [vmem(us + (3, RING) + block, BF), terms, vmem(us + (RING,) + block, F32), vmem(us + (3,) + block, BF)]
        scratch += [vmem(us + (RING, PAD, width), t) for t in (BF, F32)] + [vmem(us + (3, PAD, width), BF)]
        scratch += [dma(us + (PHASES * COPIES,))] * 2 + [dma(us + (4, 2))]
    scratch += [vmem((ZROWS + 8, GATE.width), F32), vmem((PAD + 8, HG), F32)] + [vmem((2, 16, HG), BF)] * 3
    return scratch + [vmem((2, DROWS, HD), BF), vmem((DROWS, HD), BF)] + [dma((3,))] * 2 + [dma((7,))]


ROWS_OUT = [out((2, 16, FF), BF), out((DROWS, D), BF), out((8, 128), F32)]
DOWN_BLOCKS = (GOT + 1, RING, RING, RING, PAIR, DROWS, HD)


def all_peers(here):
    return [here.moved(d, r) for d in (X, Y, Z) for r in range(1, RING)] + [here.moved(CORE)]


def over_all(here, total, nb, nr, send, recv):
    n = 0
    for stage, dim in enumerate((CORE, Z, Y, X)):
        nb[stage] = total
        copies = []
        for r in range(1, len(here.at[dim])):
            copies.append(remote(nb.at[stage], nr.at[n], send.at[n], recv.at[n], here.moved(dim, r)))
            copies[-1].start()
            n += 1
        for i, cp in enumerate(copies):
            cp.wait()
            total = total + nr[n - len(copies) + i]
    return total


def back_kernel(d, h1, dy, wg, wu, wd, by_gate, by_up, hid, pg, pd, od0, opd, gg, gd, osq, dx, nb, sem, *refs):
    here = Place()
    n = len(DOWN_SCRATCH)
    sums = Sums(here, pg, pd, refs[n:])
    meet(all_peers(here))
    step = lambda n, streams: lambda: sums.step(n, *streams)
    early, late = zip(sums.down, sums.gate[:1] + sums.upper[:1], sums.gate[1:] + sums.upper[1:])
    sums.begin(early + late)

    def states(vd, vw, wsem):
        n = D // NT
        tiles = [Loaded(n, lambda i, w=w: w.at[1, at(i, NT), :], vw.at[k], wsem.at[k]) for k, w in enumerate((wg, wu))]
        loads = []
        for k in BOTH:
            loads += fetch([(d.at[k], vd.at[k])], sem.at[pl.ds(k, 1)])
            tiles[k].start()

        def body(i):
            k, i = lax.div(i, n), lax.rem(i, n)
            for which in BOTH:
                pl.when(k == which)(lambda: tiles[which].ready(i))
            before = jnp.where(k == 0, 0.0, up(dx[:, at(i, NT)]))
            dx[:, at(i, NT)] = (before + up(mm(vd[k], vw[k, odd(i)], 1).astype(BF))).astype(BF)

        hooks = [(n - 1, loads[1].wait), (n // 2, step(0, early)), (n + 1, step(0, late))]
        loads[0].wait()
        tiled(2 * n, body, hooks)

    pl.run_scoped(states, vmem((2, T, FF), BF), vmem((2, 2, NT, FF), BF), PAIRS_SEM)

    def norm_back(vh, vy):
        for cp in fetch([(h1, vh), (dy, vy)], sem):
            cp.wait()

        def rows(i):
            r = at(i, NT)
            wide, da = up(vh[r]), up(dx[r])
            scale = lax.rsqrt(jnp.mean(wide**2, -1, keepdims=True) + 1e-6)
            mean = jnp.mean(da * wide, -1, keepdims=True)
            back = (da * scale - wide * (scale * scale * scale * mean)).astype(BF)
            dx[r] = (up(vy[r]) + up(back)).astype(BF)

        tiled(T // NT, rows)

    pl.run_scoped(norm_back, STATES, STATES)

    def hidden_back(vw, wsem, vf, fsem, vo, outsem):
        n = FF // WIDE
        tiles = [Loaded(n, lambda i: wd.at[0, at(i, WIDE), :], vw, wsem)]
        tiles += [Loaded(n, lambda i, f=f: f.at[:, at(i, WIDE)], vf.at[k], fsem.at[k]) for k, f in enumerate((by_gate, by_up))]
        outs = [Stored(lambda i, k=k: od0.at[k, :, at(i, WIDE)], vo.at[k], outsem.at[k]) for k in BOTH]
        for t in tiles:
            t.start()

        def body(i):
            slot, *_ = [t.take(i) for t in tiles]
            for o in outs:
                o.free(i)

            def rows(r):
                dhid = up(mm(dx[r], vw[slot], 1).astype(BF))
                for k in BOTH:
                    vo[k, slot, r] = (dhid * vf[k, slot, r]).astype(BF)

            in_pairs(rows)
            for o in outs:
                o.copy(i).start()

        tiled(n, body, [(2, step(1, early)), (5, step(1, late))])
        for o in outs:
            o.end(n)

    pl.run_scoped(hidden_back, vmem((2, WIDE, D), BF), PAIR_SEM, vmem((2, 2, T, WIDE), F32), PAIRS_SEM, vmem((2, 2, T, WIDE), BF), PAIRS_SEM)

    def last(*tile_refs):
        steps = [step(n, streams) for n in (2, 3, 4) for streams in (early, late)]
        DownProduct(here, hid, *tile_refs, *refs[:n]).run(dx, opd, list(enumerate(steps)))

    pl.run_scoped(last, *HIDDEN)
    nb[...] = sum(sums.last(u) for u in (2, 0, 1))
    sums.results(gg, gd)
    sums.put(nb, osq)
    sums.drain()


def back(*args):
    *ins, pg, pd = args
    outs = [out((2, T, FF), BF), DOWN_SUMS] + ROWS_OUT
    scratch = [STATES, LANES, PAIR_SEM] + DOWN_SCRATCH + sums_scratch(False)
    return call(back_kernel, outs, [HBM] * len(args), scratch, "back", ident=2)(*ins, pg, pd.reshape(DOWN_BLOCKS))


def end_kernel(a, d, pd, sq, gg, gd, osq, va, vsq, nb, nr, nsend, nrecv, sem, *refs):
    here = Place()
    n = len(COLUMNS + GATE_SCRATCH)
    gates = GateProducts(here, d, *refs[:n])
    sums = Sums(here, gates.terms, pd, refs[n:])
    a_here, sq_here = fetch([(a, va), (sq, vsq)], sem)
    meet(all_peers(here))
    sums.begin(sums.down)
    a_here.wait()
    (d0, d1), (g0, g1), (u0, u1) = sums.down, sums.gate, sums.upper

    def begin(new, *old):
        sums.begin([new])
        sums.step(0, *old)

    hooks = {2: lambda: begin(g0, d0), 3: lambda: begin(g1, d1), 5: lambda: sums.step(0, g0, g1), 6: lambda: sums.begin([u0])}
    gates.run(va, hooks.items())
    sums.begin([u1])
    sums.step(1, g0, d0, g1)
    sums.step(0, u0)
    sums.step(1, d1)
    sums.step(0, u1)
    for n in (2, 3):
        sums.step(n, g0, d0, g1, d1)
    sums.step(1, u0, u1)
    sums.step(4, g0, d0, g1, d1)
    sums.step(2, u0, u1)
    total = sums.last(2) + sums.last(0)
    for n in (3, 4):
        sums.step(n, u0, u1)
    total += sums.last(1)
    sq_here.wait()
    nb[4] = over_all(here, total + vsq[...], nb, nr, nsend, nrecv)
    sums.put(nb.at[4], osq)
    sums.results(gg, gd)
    sums.drain()


def end(a, d, pd, sq):
    scratch = [STATES, LANES, vmem((5, 8, 128), F32), vmem((10, 8, 128), F32)] + [dma((10,))] * 2 + [PAIR_SEM]
    scratch += COLUMNS + GATE_SCRATCH + sums_scratch(True)
    return call(end_kernel, ROWS_OUT, [HBM] * 4, scratch, "end", ident=4)(a, d, pd.reshape(DOWN_BLOCKS), sq)


COUNT = 3 * L * D * FF


def adamw_kernel(gg0, gg1, gd0, gd1, norm, *refs):
    old, (wg, wu, wd), new, (ng, nd, win, wind, sg, sw, sem) = refs[:6], refs[6:9], refs[9:15], refs[15:]
    i = lax.axis_index("dp")
    start, off = pl.multiple_of(i * ROWS // 8 * 8, 8), i * ROWS % 8
    copies = [pltpu.make_async_copy((wg, wu)[u // L].at[u % L, pl.ds(start, 16), :], win.at[u], sem.at[u]) for u in range(PAIR * L)]
    copies.append(pltpu.make_async_copy(wd.at[:, pl.ds(pl.multiple_of(i * DROWS, 8), DROWS), :], wind, sem.at[PAIR * L]))
    for cp in copies:
        cp.start()
    factor = jnp.minimum(1.0, 0.5 * lax.rsqrt(jnp.full((1, 1), jnp.sum(norm[...])) / COUNT + 1e-30))
    for cp in copies:
        cp.wait()

    def step(k, w, g):
        g = g * factor
        m = 0.9 * old[k][...] + 0.1 * g
        v = 0.95 * old[k + 3][...] + 0.05 * g * g
        new[k][...], new[k + 3][...] = m, v
        return w - 0.02 * (m * lax.rsqrt(v + 1e-8) + 0.1 * w)

    for k in BOTH:
        for l in BOTH:
            w = up(win[k * L + l])
            rows = w[0:ROWS]
            for skip in (2, 4, 6):
                rows = jnp.where(off == skip, w[skip : skip + ROWS], rows)
            sw[:, l, :] = rows
            sg[:, l, :] = up((gg0, gg1)[l][k])[0:ROWS]
        sw[...] = step(k, sw[...], sg[...])
        for l in BOTH:
            ng[k * L + l, 0:ROWS] = sw[:, l, :].astype(BF)
    nd[...] = step(2, up(wind[...]), jnp.stack([up(gd0[...]), up(gd1[...])])).astype(BF)


def adamw(sums, norm, moments, weights):
    weights = [pltpu.with_memory_space_constraint(w, pltpu.HBM) for w in weights]
    flip = lambda k, t: t if k % 3 == 2 else jnp.swapaxes(t, 0, 1)
    moments = [flip(k, t) for k, t in enumerate(moments)]
    outs = [out(t.shape, F32) for t in moments] + [vmem((PAIR * L, 16, FF), BF), vmem((L, DROWS, D), BF)]
    scratch = [vmem((PAIR * L, 16, FF), BF), vmem((L, DROWS, D), BF)] + [vmem((ROWS, L, FF), F32)] * 2 + [dma((PAIR * L + 1,))]
    *new, ng, nd = call(adamw_kernel, outs, [VM] * 11 + [HBM] * 3, scratch, "adamw", MOST - 5 * 2**17, out_specs=[VM] * 8)(*sums, norm, *moments, *weights)
    return [flip(k, t) for k, t in enumerate(new)], ng, nd


class Gathered:
    def __init__(self, here, cut, refs, b, u, s):
        self.here, self.cut, self.refs, self.b, self.u, self.s = here, cut, refs, b, u, s
        self.order = cut.dims(s)[::-1]
        n, first = (HG, s * cut.width) if cut.gate else (HD, 0)
        self.whole = [pl.ds(pl.multiple_of(c * n + first, 128), cut.width) for c in here.at[CORE]]

    def ref(self, at):
        return self.refs[self.u // L].at[(self.u % L,) + at]

    def copy(self, phase, k):
        dim, back = self.order[phase], k % 2
        cols = self.whole[0]
        if k >= 2:
            cols = self.cut.part(self.s, back, cols.start)
        v = self.ref(self.cut.index(self.here, self.s, dim, 0 if k < 2 else 2 * back - 1, self.order[:phase], cols))
        i = phase * 4 + k
        return remote(v, v, self.b[0].at[self.u, self.s, i], self.b[1].at[self.u, self.s, i], self.here.moved(dim, 1 - 2 * back))

    def across(self, r, core=0):
        v = self.ref(self.cut.index(self.here, self.s, self.order[2], r, self.order, self.whole[core]))
        i = PHASES * 4 + r % RING
        return remote(v, v, self.b[0].at[self.u, self.s, i], self.b[1].at[self.u, self.s, i], self.here.moved(CORE))

    def start(self, phase):
        for k in BOTH:
            self.copy(phase, k).start()
        if phase == 2:
            self.across(0).start()

    def forward(self, phase):
        for k in BOTH:
            self.copy(phase, k).wait_recv()
            self.copy(phase, 2 + k).start()
            if phase == 2:
                self.across(2 * k - 1).start()

    def end(self, phase):
        for k in BOTH:
            self.copy(phase, 2 + k).wait_recv()
        if phase < 2:
            self.start(phase + 1)
        else:
            self.across(2).start()


def ag_kernel(wg, wd, o0, o1, od, cs, cx, zb, zf, zm, csend, crecv, zsend, zrecv, gsend, grecv, dsend, drecv):
    here = Place()
    (x, y, z, c), other = (steps[0] for steps in here.at), here.moved(CORE)
    meet([here.moved(d, r) for d in (X, Y, Z) for r in (1, -1)] + [other])
    half = lambda which, n: pl.ds(pl.multiple_of(which * n, 128), n)
    mine, theirs = c, 1 - c

    def swap_g(u):
        return remote(wg.at[u, :, half(theirs, HG)], cx.at[u], csend.at[u], crecv.at[u], other)

    def swap_d(l, core, which):
        there = od.at[l, x, y, z, core, :, half(which, HD)]
        return remote(wd.at[l, :, half(theirs, HD)], there, csend.at[PAIR * L + l], crecv.at[PAIR * L + l], other)

    for u in range(PAIR * L):
        swap_g(u).start()
    for l in BOTH:
        swap_d(l, c, theirs).start()
        od[l, x, y, z, c, :, half(mine, HD)] = wd[l, :, half(mine, HD)]

    def zcopy(s, k):
        back = k % 2
        cols = GATE.part(s, back, s * GATE.width) if k >= 2 else pl.ds(s * GATE.width, GATE.width)
        v = zb.at[here.at[Z][0 if k < 2 else (2 * back - 1) % RING], :, cols]
        return remote(v, v, zsend.at[s, k], zrecv.at[s, k], here.moved(Z, 1 - 2 * back))

    for u in range(PAIR * L):
        swap_g(u).wait_recv()
        own, got = up(wg[u, :, half(mine, HG)]), up(cx[u])
        for core in range(PAIR):
            row = (u * PAIR + core) * ROWS
            cs[row : row + ROWS] = jnp.where(c == core, own, got)[0:ROWS]
    for s in BOTH:
        cols = slice(s * GATE.width, (s + 1) * GATE.width)
        zb[z, :, cols] = cs[:, cols].astype(BF)
        for k in BOTH:
            zcopy(s, k).start()
    gate = [Gathered(here, GATE, (o0, o1), (gsend, grecv), u, s) for u in range(PAIR * L) for s in BOTH]
    down = [Gathered(here, DOWN, (od,), (dsend, drecv), l, s) for l in BOTH for s in BOTH]
    for l in BOTH:
        swap_d(l, 1 - c, mine).wait_recv()
    for st in down:
        st.start(0)
    for s in BOTH:
        for k in BOTH:
            zcopy(s, k).wait_recv()
            zcopy(s, 2 + k).start()
    for st in down:
        st.forward(0)

    for s in BOTH:
        cols = slice(s * GATE.width, (s + 1) * GATE.width)
        for k in range(2, 4):
            zcopy(s, k).wait_recv()
        for i in range(RING):
            zm[...] = up(zb[i, :, cols])
            for u in range(PAIR * L):
                n = PAIR * ROWS
                zf[u, i * n : i * n + n] = zm[u * n : u * n + n]
        for st in gate[s::2]:
            (o0, o1)[st.u // L][st.u % L, x, y, 0, :, st.whole[0]] = zf[st.u].astype(BF)
            st.start(1)
    for st in down:
        st.end(0)
    both = gate[: L * 2] + down[:2] + gate[L * 2 :] + down[2:]
    for phase in (1, 2):
        for st in both:
            st.forward(phase)
        for st in both:
            st.end(phase)
    for u in range(PAIR * L):
        swap_g(u).wait_send()
    for l in BOTH:
        swap_d(l, c, theirs).wait_send()
    for s in BOTH:
        for k in range(4):
            zcopy(s, k).wait_send()
    for st in both:
        for phase in range(1 if st.cut.gate else 0, PHASES):
            for k in range(4):
                st.copy(phase, k).wait_send()
        for r in range(RING):
            st.across(r).wait_send()
            st.across(r, 1).wait_recv()


def ag(wg, wd):
    block = (RING, RING, 1, ZROWS, FF)
    outs = [pltpu.VMEM((L,) + block, BF)] * 2 + [pltpu.VMEM((L, RING, RING, RING, PAIR, DROWS, D), BF)]
    n, sems = PAIR * L, PHASES * 4 + RING
    scratch = [vmem((ZROWS, HG), F32), vmem((n, 16, HG), BF), vmem((RING, ZROWS, HG), BF), vmem((n, ZROWS, GATE.width), F32), vmem((ZROWS, GATE.width), F32)]
    scratch += [dma((n + L,))] * 2 + [dma((2, 4))] * 2 + [dma((n, 2, sems))] * 2 + [dma((L, 2, sems))] * 2
    return call(ag_kernel, outs, [VM] * 2, scratch, "ag", vmem_limit=5 * 2**20, ident=3, out_specs=[VM] * 3)(wg, wd)


def put_kernel(src, dst, sem):
    copies = [pltpu.make_async_copy(src.at[l, x], dst.at[l, x], sem.at[l, x]) for l in BOTH for x in range(RING)]
    for cp in copies:
        cp.start()
    for cp in copies:
        cp.wait()


def put(w):
    return call(put_kernel, [out(w.shape, BF)], [VM], [dma((L, RING))], "put", vmem_limit=2**20)(w)[0]


def device_step(x, dy, wg, wu, wd, *moments):
    x, dy = x[0], dy[0]
    a0, hid0, by_gate, by_up, h1, a1, hid1, d1 = forward(x, dy, wg, wu, wd)
    d0, pd0, gg1, gd1, squares1 = back(d1, h1, dy, wg, wu, wd, by_gate, by_up, hid0, *dw(a1, d1, hid1, dy))
    gg0, gd0, norm = end(a0, d0, pd0, squares1)
    moments, ng, nd = adamw((gg0, gg1, gd0, gd1), norm, moments, (wg, wu, wd))
    return (*(put(new).reshape(w.shape) for new, w in zip(ag(ng, nd), (wg, wu, wd))), *moments)


def solution(mesh):
    rows, moment, whole = P(("rep", "dp"), None, None), P(None, "dp", None), P(None, None, None)
    return jax.shard_map(
        device_step,
        mesh=mesh,
        in_specs=(rows,) * 2 + (whole,) * 3 + (moment,) * 6,
        out_specs=(P("rep", None, None),) * 3 + (P("rep", "dp", None),) * 6,
        check_vma=False,
    )
```

time: 492 us -> 414 us (0.84); the launches traced: 484 us -> 413 us
  matrix products: 141 us -> 0 us
  Pallas kernels: 332 us -> 412 us
  other arithmetic: 6.37 us -> 0 us
    dot_general x9 -> x0, matrix products: 141 us -> none  [mm(): lax.dot_general(a, b, (((1,), (across,)), ((), ())), preferred_element_ty...]
    pallas_call x7 -> x8, Pallas kernels: 219 us -> 299 us  [the longest x1 83.4 us: end(): call(end_kernel, ROWS_OUT, [HBM] * 4, scratch, 'end', ident=4)]
where the time goes in v2:
time: 414 us; the launch traced here: 413 us
  Pallas kernels  412 us (100%)
    pallas_call x1, Pallas kernels, ag(): call(ag_kernel, outs, [VM] * 2, scratch, 'ag', vmem_limit=5 * 2 ** 20, id...  113 us
    pallas_call x1, Pallas kernels, end(): call(end_kernel, ROWS_OUT, [HBM] * 4, scratch, 'end', ident=4)  83.4 us
    pallas_call x1, Pallas kernels, back(): call(back_kernel, outs, [HBM] * len(args), scratch, 'back', ident=2)  81.1 us
    pallas_call x1, Pallas kernels, forward(): call(forward_kernel, outs, [HBM] * 5, scratch, 'forward')(x, dy, wg, wu, wd)  70.8 us
    pallas_call x1, Pallas kernels, dw(): call(dw_kernel, [GATE_SUMS, DOWN_SUMS], [HBM] * 4, scratch, 'dw', ident=1)  41.7 us
    pallas_call x3, Pallas kernels, put(): call(put_kernel, [out(w.shape, BF)], [VM], [dma((L, RING))], 'put', vmem_...  16.9 us

profile of v2, /device:TPU:1, one launch (start us, length us, event | category | flops | bytes accessed | tf_op | source)
XLA Modules:
  0.0 413.1 jit_solution(7522968605382801654)
XLA Ops:
  0.6 70.8 %forward.1 = (bf16[1024,1280]{1,0:T(8,128)(2,1)}, bf16[1024,3072]{1,0:T(8,128)(2,1)}, f32[1024,3072]{1,0:T(8,128)}, f32[1024,3072]{1,0:T(8,128)}, bf16[1024,1280...) custom-call(bf16[1024,1280]{1,0:T(8,128)(2,1)} %bitcast.23, ...), custom_call_target="tpu_custom_call" | custom-call | tf_op jit(solution)/shard_map/forward/pallas_call | solution.py:293
  71.5 41.7 %dw.1 = (bf16[3,2,4,4,1,80,1536]{6,5,4,3,2,1,0:T(8,128)(2,1)}, bf16[3,3072,640]{2,1,0:T(8,128)(2,1)}) custom-call(bf16[1024,1280]{1,0:T(8,128)(2,1)} %get-tuple-element.44.a, bf16[2,1024,3072]{2,1,0:T(8,128)(2,1)} %get-tuple-element.39.d, bf16[1024,3072]{1,0:T(8,128)(2,1)} %get-tuple-element.45.hid, bf16[1024,1280]{1,0:T(8,128)(2,1)} %bitcast.16), custom_call_target="tpu_custom_call" | custom-call | tf_op jit(solution)/shard_map/dw/pallas_call | solution.py:414
  113.2 81.1 %back.1 = (bf16[2,1024,3072]{2,1,0:T(8,128)(2,1)}, bf16[3,3072,640]{2,1,0:T(8,128)(2,1)}, bf16[2,16,3072]{2,1,0:T(8,128)(2,1)}, bf16[24,1280]{1,0:T(8,128)(2,1)}, f32[8,128]{1,0:T(8,128)}) custom-call(bf16[2,1024,3072]{2,1,0:T(8,128)(2,1)} %get-tuple-element.39.d, bf16[1024,1280]{1,0:T(8,128)(2,1)} %get-tuple-element.40.h1, bf16[1024,1280]{1,0:T(8,128)(2,1)} %bitcast.17, ...), custom_call_target="tpu_custom_call" | custom-call | tf_op jit(solution)/shard_map/back/pallas_call | solution.py:744
  194.3 83.4 %end.1 = (bf16[2,16,3072]{2,1,0:T(8,128)(2,1)}, bf16[24,1280]{1,0:T(8,128)(2,1)}, f32[8,128]{1,0:T(8,128)}) custom-call(bf16[1024,1280]{1,0:T(8,128)(2,1)} %get-tuple-element.38.a, bf16[2,1024,3072]{2,1,0:T(8,128)(2,1)} %get-tuple-element.48.d, bf16[3,4,4,4,2,24,640]{6,5,4,3,2,1,0:T(8,128)(2,1)} %bitcast.21, f32[8,128]{1,0:T(8,128)} %get-tuple-element.50.sq), custom_call_target="tpu_custom_call" | custom-call | tf_op jit(solution)/shard_map/end/pallas_call | solution.py:788
  277.8 5.2 %adamw.1 = (f32[10,2,3072]{2,1,0:T(2,128)}, f32[10,2,3072]{2,1,0:T(2,128)}, f32[2,24,1280]{2,1,0:T(8,128)}, f32[10,2,3072]{2,1,0:T(2,128)}, f32[10,2,3072]{2,1,0...) custom-call(bf16[2,16,3072]{2,1,0:T(8,128)(2,1)} %get-tuple-element.51.gg0, ...), custom_call_target="tpu_custom_call" | custom-call | tf_op jit(solution)/shard_map/adamw/pallas_call | solution.py:833
  283.0 112.9 %ag.1 = (bf16[2,4,4,1,80,3072]{5,4,3,2,1,0:T(8,128)(2,1)S(1)}, bf16[2,4,4,1,80,3072]{5,4,3,2,1,0:T(8,128)(2,1)S(1)}, bf16[2,4,4,4,2,24,1280]{6,5,4,3,2,1,0:T(8,128)(2,1)S(1)}) custom-call(bf16[4,16,3072]{2,1,0:T(8,128)(2,1)S(1)} %get-tuple-element.56.wg, bf16[2,24,1280]{2,1,0:T(8,128)(2,1)S(1)} %get-tuple-element.57.wd), custom_call_target="tpu_custom_call" | custom-call | tf_op jit(solution)/shard_map/ag/pallas_call | solution.py:975
  395.9 5.6 %put.3 = bf16[2,4,4,1,80,3072]{5,4,3,2,1,0:T(8,128)(2,1)} custom-call(bf16[2,4,4,1,80,3072]{5,4,3,2,1,0:T(8,128)(2,1)S(1)} %get-tuple-element.58.src), custom_call_target="tpu_custom_call" | custom-call | tf_op jit(solution)/shard_map/put/pallas_call | solution.py:987
  401.6 5.6 %put.4 = bf16[2,4,4,1,80,3072]{5,4,3,2,1,0:T(8,128)(2,1)} custom-call(bf16[2,4,4,1,80,3072]{5,4,3,2,1,0:T(8,128)(2,1)S(1)} %get-tuple-element.59.src), custom_call_target="tpu_custom_call" | custom-call | tf_op jit(solution)/shard_map/put/pallas_call | solution.py:987
  407.2 5.6 %put.5 = bf16[2,4,4,4,2,24,1280]{6,5,4,3,2,1,0:T(8,128)(2,1)} custom-call(bf16[2,4,4,4,2,24,1280]{6,5,4,3,2,1,0:T(8,128)(2,1)S(1)} %get-tuple-element.60.src), custom_call_target="tpu_custom_call" | custom-call | tf_op jit(solution)/shard_map/put/pallas_call | solution.py:987

commit v3 on v2

--- a/solution.py
+++ b/solution.py
@@ -148,15 +148,109 @@
     return 1 if k in (0, 3, 4) else -1
 
 
+SUM, OWN, GOT = range(3)
+TILES = 6
+TILE = FF // TILES
+DOWN_SCRATCH = [vmem((TILES, TILE, HD), BF)] + [dma((TILES,))] * 2 + [dma((GOT + 1, TILES))]
+HIDDEN = [vmem((2, T, TILE), BF), PAIR_SEM, vmem((TILES, PAIR, TILE, HD), BF)]
+BLOCKS = (RING, RING, 1, ZROWS)
+GATE_SCRATCH = [vmem((2, 2) + BLOCKS + (GATE.width,), BF)] * 3 + [PAIRS_SEM] * 2
+GATE_SUMS, DOWN_SUMS = out((GOT + 1, 2) + BLOCKS + (HG,), BF), out((GOT + 1, FF, HD), BF)
+
+
+class DownProduct:
+    def __init__(self, here, hid, hbuf, hsem, halves, got, send, recv, outsem):
+        self.here, self.halves, self.got, self.send, self.recv, self.outsem = here, halves, got, send, recv, outsem
+        self.hidden = Loaded(TILES, lambda i: hid.at[:, at(i, TILE)], hbuf, hsem)
+        self.hidden.start()
+
+    def swap(self, i):
+        _, theirs = self.here.at[CORE]
+        return remote(self.halves.at[i, theirs], self.got.at[i], self.send.at[i], self.recv.at[i], self.here.moved(CORE))
+
+    def put(self, od, i):
+        mine, theirs = self.here.at[CORE]
+        srcs = self.halves.at[i, theirs], self.halves.at[i, mine], self.got.at[i]
+        return [pltpu.make_async_copy(src, od.at[k, at(i, TILE), :], self.outsem.at[k, i]) for k, src in enumerate(srcs)]
+
+    def run(self, dy, od, hooks=()):
+        mine, theirs = self.here.at[CORE]
+
+        def add(i):
+            self.swap(i).wait()
+            self.halves[i, theirs] = (up(self.got[i]) + up(self.halves[i, mine])).astype(BF)
+            for cp in self.put(od, i):
+                cp.start()
+
+        def body(i):
+            full = tn(self.hidden.buf[self.hidden.take(i)], dy[...])
+            for half in BOTH:
+                self.halves[i, half] = full[:, half * HD : (half + 1) * HD]
+            self.swap(i).start()
+            pl.when(i > 0)(lambda: add(i - 1))
+
+        tiled(TILES, body, hooks)
+        add(TILES - 1)
+        for i in range(TILES):
+            for cp in self.put(od, i):
+                cp.wait()
+
+
+class GateProducts:
+    def __init__(self, here, d, buf, sem, total, own, got, send, recv):
+        self.here, self.sems = here, (send, recv)
+        self.terms = total, own, got
+
+        def src(i):
+            t, (mine, theirs) = lax.rem(i, 4), here.at[CORE]
+            return d.at[lax.div(i, 4), :, at(odd(i), GATE.width, jnp.where(t < 2, theirs, mine) * HG)]
+
+        self.tiles = Loaded(8, src, buf, sem)
+        self.tiles.start()
+
+    def swap(self, w, t):
+        send, recv = self.sems
+        return remote(self.terms[SUM].at[w, t], self.terms[GOT].at[w, t], send.at[w, t], recv.at[w, t], self.here.moved(CORE))
+
+    def put(self, og, sem, w, t):
+        return [pltpu.make_async_copy(v.at[w, t], og.at[k, w, :, :, :, :, at(t, GATE.width)], sem.at[k, w, t]) for k, v in enumerate(self.terms)]
+
+    def run(self, a, hooks=(), after=lambda w, t: None):
+        total, own, got = self.terms
+
+        def product(i):
+            return tn(a[...], self.tiles.buf[self.tiles.take(i)]).reshape(BLOCKS + (GATE.width,))
+
+        def matrix(w, _):
+            def theirs(t):
+                total[w, t] = product(4 * w + t)
+                self.swap(w, t).start()
+
+            def mine(t):
+                own[w, t] = product(4 * w + 2 + t)
+                self.swap(w, t).wait()
+                total[w, t] = (up(got[w, t]) + up(own[w, t])).astype(BF)
+                after(w, t)
+
+            tiled(2, theirs, hooks, 4 * w)
+            tiled(2, mine, hooks, 4 * w + 2)
+            return _
+
+        lax.fori_loop(0, 2, matrix, 0)
+
+
+COLUMNS = [vmem((2, T, GATE.width), BF), PAIR_SEM]
+
+
 PART = T // 4
 
 
-def in_pairs(body):
-    def both(i):
-        for k in BOTH:
-            body(at(2 * i + k, PART))
-
-    tiled(T // (2 * PART), both)
+def in_parts(body, at_once=T // PART):
+    def some(i):
+        for k in range(at_once):
+            body(at(at_once * i + k, PART))
+
+    tiled(T // (at_once * PART), some)
 
 
 def normed(src, dst):
@@ -194,8 +288,9 @@
 STATES = vmem((T, D), BF)
 
 
-def forward_kernel(x, dy, wg, wu, wd, oa0, ohid0, ofg, ofu, oh1, oa1, ohid1, od1, vx, va, vhid, vdy, sem, osem, hsem):
-    n = FF // WIDE
+def forward_kernel(x, dy, wg, wu, wd, oa0, ohid0, ofg, ofu, oh1, ohid1, od1, og, od, vx, va, vhid, vdy, sem, osem, hsem, *refs):
+    n, here = FF // WIDE, Place()
+    meet([here.moved(CORE)])
     x_here, dy_here = fetch([(x, vx), (dy, vdy)], sem)
     wide = lambda ref, l: lambda i: ref.at[l, :, at(i, WIDE)]
 
@@ -221,7 +316,7 @@
                 for k in BOTH:
                     vo[k, slot, r] = factors[k]
 
-            in_pairs(rows)
+            in_parts(rows)
             put(i).start()
             for o in outs:
                 o.copy(i).start()
@@ -243,7 +338,7 @@
             def rows(r):
                 vx[r, cols] = (up(vx[r, cols]) + up(mm(vhid[r], vw[slot]).astype(BF))).astype(BF)
 
-            in_pairs(rows)
+            in_parts(rows)
 
         tiled(D // NT, body)
 
@@ -258,7 +353,7 @@
         for t in tiles:
             t.start()
         normed(vx, va)
-        kept = fetch([(vx, oh1), (va, oa1)], osem)
+        kept = fetch([(vx, oh1)], osem)
         dy_here.wait()
 
         def body(i):
@@ -273,7 +368,7 @@
                 for k in BOTH:
                     vo[k, slot, r] = (dhid * factors[k]).astype(BF)
 
-            in_pairs(rows)
+            in_parts(rows)
             for o in outs:
                 o.copy(i).start()
 
@@ -285,133 +380,33 @@
 
     pl.run_scoped(third, HALVES, PAIRS_SEM, vmem((2, WIDE, D), BF), PAIR_SEM, vmem((3, 2, T, WIDE), BF), dma((3, 2)))
 
+    def fourth(*local):
+        k = len(HIDDEN)
+        down = DownProduct(here, ohid1, *local[:k], *refs[: len(DOWN_SCRATCH)])
+        *gate_refs, gsem = refs[len(DOWN_SCRATCH) :]
+        gates = GateProducts(here, od1, *local[k:], *gate_refs)
+
+        def put(w, t):
+            for cp in gates.put(og, gsem, w, t):
+                cp.start()
+
+        down.run(vdy, od)
+        gates.run(va, after=put)
+        for w in BOTH:
+            for t in BOTH:
+                for cp in gates.put(og, gsem, w, t):
+                    cp.wait()
+
+    pl.run_scoped(fourth, *HIDDEN, *COLUMNS, *GATE_SCRATCH[:GOT])
+
 
 def forward(x, dy, wg, wu, wd):
     states, hidden = out((T, D), BF), out((T, FF), BF)
-    outs = [states, hidden, out((T, FF), F32), out((T, FF), F32), states, states, hidden, out((2, T, FF), BF)]
+    outs = [states, hidden, out((T, FF), F32), out((T, FF), F32), states, hidden, out((2, T, FF), BF), GATE_SUMS, DOWN_SUMS]
     scratch = [STATES] * 2 + [vmem((T, FF), BF), STATES, PAIR_SEM, PAIR_SEM, dma((FF // WIDE,))]
-    return call(forward_kernel, outs, [HBM] * 5, scratch, "forward")(x, dy, wg, wu, wd)
-
-
-SUM, OWN, GOT = range(3)
-TILES = 6
-TILE = FF // TILES
-DOWN_SCRATCH = [vmem((TILES, TILE, HD), BF)] + [dma((TILES,))] * 2 + [dma((GOT + 1, TILES))]
-HIDDEN = [vmem((2, T, TILE), BF), PAIR_SEM, vmem((TILES, PAIR, TILE, HD), BF)]
-BLOCKS = (RING, RING, 1, ZROWS)
-GATE_SCRATCH = [vmem((2, 2) + BLOCKS + (GATE.width,), BF)] * 3 + [PAIRS_SEM] * 2
-GATE_SUMS, DOWN_SUMS = out((GOT + 1, 2) + BLOCKS + (HG,), BF), out((GOT + 1, FF, HD), BF)
-
-
-class DownProduct:
-    def __init__(self, here, hid, hbuf, hsem, halves, got, send, recv, outsem):
-        self.here, self.halves, self.got, self.send, self.recv, self.outsem = here, halves, got, send, recv, outsem
-        self.hidden = Loaded(TILES, lambda i: hid.at[:, at(i, TILE)], hbuf, hsem)
-        self.hidden.start()
-
-    def swap(self, i):
-        _, theirs = self.here.at[CORE]
-        return remote(self.halves.at[i, theirs], self.got.at[i], self.send.at[i], self.recv.at[i], self.here.moved(CORE))
-
-    def put(self, od, i):
-        mine, theirs = self.here.at[CORE]
-        srcs = self.halves.at[i, theirs], self.halves.at[i, mine], self.got.at[i]
-        return [pltpu.make_async_copy(src, od.at[k, at(i, TILE), :], self.outsem.at[k, i]) for k, src in enumerate(srcs)]
-
-    def run(self, dy, od, hooks=()):
-        mine, theirs = self.here.at[CORE]
-
-        def add(i):
-            self.swap(i).wait()
-            self.halves[i, theirs] = (up(self.got[i]) + up(self.halves[i, mine])).astype(BF)
-            for cp in self.put(od, i):
-                cp.start()
-
-        def body(i):
-            full = tn(self.hidden.buf[self.hidden.take(i)], dy[...])
-            for half in BOTH:
-                self.halves[i, half] = full[:, half * HD : (half + 1) * HD]
-            self.swap(i).start()
-            pl.when(i > 0)(lambda: add(i - 1))
-
-        tiled(TILES, body, hooks)
-        add(TILES - 1)
-        for i in range(TILES):
-            for cp in self.put(od, i):
-                cp.wait()
-
-
-class GateProducts:
-    def __init__(self, here, d, buf, sem, total, own, got, send, recv):
-        self.here, self.sems = here, (send, recv)
-        self.terms = total, own, got
-
-        def src(i):
-            t, (mine, theirs) = lax.rem(i, 4), here.at[CORE]
-            return d.at[lax.div(i, 4), :, at(odd(i), GATE.width, jnp.where(t < 2, theirs, mine) * HG)]
-
-        self.tiles = Loaded(8, src, buf, sem)
-        self.tiles.start()
-
-    def swap(self, w, t):
-        send, recv = self.sems
-        return remote(self.terms[SUM].at[w, t], self.terms[GOT].at[w, t], send.at[w, t], recv.at[w, t], self.here.moved(CORE))
-
-    def put(self, og, sem, w, t):
-        return [pltpu.make_async_copy(v.at[w, t], og.at[k, w, :, :, :, :, at(t, GATE.width)], sem.at[k, w, t]) for k, v in enumerate(self.terms)]
-
-    def run(self, a, hooks=(), after=lambda w, t: None):
-        total, own, got = self.terms
-
-        def product(i):
-            return tn(a[...], self.tiles.buf[self.tiles.take(i)]).reshape(BLOCKS + (GATE.width,))
-
-        def matrix(w, _):
-            def theirs(t):
-                total[w, t] = product(4 * w + t)
-                self.swap(w, t).start()
-
-            def mine(t):
-                own[w, t] = product(4 * w + 2 + t)
-                self.swap(w, t).wait()
-                total[w, t] = (up(got[w, t]) + up(own[w, t])).astype(BF)
-                after(w, t)
-
-            tiled(2, theirs, hooks, 4 * w)
-            tiled(2, mine, hooks, 4 * w + 2)
-            return _
-
-        lax.fori_loop(0, 2, matrix, 0)
-
-
-COLUMNS = [vmem((2, T, GATE.width), BF), PAIR_SEM]
-
-
-def dw_kernel(a, d, hid, dy, og, od, va, vy, sem, gout, *refs):
-    here = Place()
-    n = len(HIDDEN + DOWN_SCRATCH)
-    down = DownProduct(here, hid, *refs[:n])
-    dy_here, a_here = fetch([(dy, vy), (a, va)], sem)
-    gates = GateProducts(here, d, *refs[n:])
-    meet([here.moved(CORE)])
-
-    def put(w, t):
-        for cp in gates.put(og, gout, w, t):
-            cp.start()
-
-    dy_here.wait()
-    down.run(vy, od)
-    a_here.wait()
-    gates.run(va, after=put)
-    for w in BOTH:
-        for t in BOTH:
-            for cp in gates.put(og, gout, w, t):
-                cp.wait()
-
-
-def dw(a, d, hid, dy):
-    scratch = [STATES] * 2 + [PAIR_SEM, dma((GOT + 1, 2, 2))] + HIDDEN + DOWN_SCRATCH + COLUMNS + GATE_SCRATCH
-    return call(dw_kernel, [GATE_SUMS, DOWN_SUMS], [HBM] * 4, scratch, "dw", ident=1)(a, d, hid, dy)
+    scratch += DOWN_SCRATCH + GATE_SCRATCH[GOT:] + [dma((GOT + 1, 2, 2))]
+    a0, hid0, by_gate, by_up, h1, _, d1, pg, pd = call(forward_kernel, outs, [HBM] * 5, scratch, "forward", ident=1)(x, dy, wg, wu, wd)
+    return a0, hid0, by_gate, by_up, h1, d1, pg, pd
 
 
 PHASES, COPIES = 3, 6
@@ -652,7 +647,7 @@
     return total
 
 
-def back_kernel(d, h1, dy, wg, wu, wd, by_gate, by_up, hid, pg, pd, od0, opd, gg, gd, osq, dx, nb, sem, *refs):
+def back_kernel(d, h1, dy, wg, wu, wd, by_gate, by_up, hid, pg, pd, od0, opd, gg, gd, osq, dx, vh, vy, nb, sem, state_sem, *refs):
     here = Place()
     n = len(DOWN_SCRATCH)
     sums = Sums(here, pg, pd, refs[n:])
@@ -660,6 +655,7 @@
     step = lambda n, streams: lambda: sums.step(n, *streams)
     early, late = zip(sums.down, sums.gate[:1] + sums.upper[:1], sums.gate[1:] + sums.upper[1:])
     sums.begin(early + late)
+    states_here = fetch([(h1, vh), (dy, vy)], state_sem)
 
     def states(vd, vw, wsem):
         n = D // NT
@@ -682,21 +678,16 @@
 
     pl.run_scoped(states, vmem((2, T, FF), BF), vmem((2, 2, NT, FF), BF), PAIRS_SEM)
 
-    def norm_back(vh, vy):
-        for cp in fetch([(h1, vh), (dy, vy)], sem):
-            cp.wait()
-
-        def rows(i):
-            r = at(i, NT)
-            wide, da = up(vh[r]), up(dx[r])
-            scale = lax.rsqrt(jnp.mean(wide**2, -1, keepdims=True) + 1e-6)
-            mean = jnp.mean(da * wide, -1, keepdims=True)
-            back = (da * scale - wide * (scale * scale * scale * mean)).astype(BF)
-            dx[r] = (up(vy[r]) + up(back)).astype(BF)
-
-        tiled(T // NT, rows)
-
-    pl.run_scoped(norm_back, STATES, STATES)
+    def norm_back(i):
+        r = at(i, NT)
+        wide, da = up(vh[r]), up(dx[r])
+        scale = lax.rsqrt(jnp.mean(wide**2, -1, keepdims=True) + 1e-6)
+        mean = jnp.mean(da * wide, -1, keepdims=True)
+        dx[r] = (up(vy[r]) + up((da * scale - wide * (scale * scale * scale * mean)).astype(BF))).astype(BF)
+
+    for cp in states_here:
+        cp.wait()
+    tiled(T // NT, norm_back)
 
     def hidden_back(vw, wsem, vf, fsem, vo, outsem):
         n = FF // WIDE
@@ -716,18 +707,18 @@
                 for k in BOTH:
                     vo[k, slot, r] = (dhid * vf[k, slot, r]).astype(BF)
 
-            in_pairs(rows)
+            in_parts(rows, 2)
             for o in outs:
                 o.copy(i).start()
 
-        tiled(n, body, [(2, step(1, early)), (5, step(1, late))])
+        tiled(n, body, [(1, step(1, early)), (3, step(1, late)), (4, step(2, early)), (5, step(2, late))])
         for o in outs:
             o.end(n)
 
     pl.run_scoped(hidden_back, vmem((2, WIDE, D), BF), PAIR_SEM, vmem((2, 2, T, WIDE), F32), PAIRS_SEM, vmem((2, 2, T, WIDE), BF), PAIRS_SEM)
 
     def last(*tile_refs):
-        steps = [step(n, streams) for n in (2, 3, 4) for streams in (early, late)]
+        steps = [step(n, streams) for n in (3, 4) for streams in (early, late)]
         DownProduct(here, hid, *tile_refs, *refs[:n]).run(dx, opd, list(enumerate(steps)))
 
     pl.run_scoped(last, *HIDDEN)
@@ -740,7 +731,7 @@
 def back(*args):
     *ins, pg, pd = args
     outs = [out((2, T, FF), BF), DOWN_SUMS] + ROWS_OUT
-    scratch = [STATES, LANES, PAIR_SEM] + DOWN_SCRATCH + sums_scratch(False)
+    scratch = [STATES] * 3 + [LANES, PAIR_SEM, PAIR_SEM] + DOWN_SCRATCH + sums_scratch(False)
     return call(back_kernel, outs, [HBM] * len(args), scratch, "back", ident=2)(*ins, pg, pd.reshape(DOWN_BLOCKS))
 
 
@@ -759,7 +750,7 @@
         sums.begin([new])
         sums.step(0, *old)
 
-    hooks = {2: lambda: begin(g0, d0), 3: lambda: begin(g1, d1), 5: lambda: sums.step(0, g0, g1), 6: lambda: sums.begin([u0])}
+    hooks = {2: lambda: begin(g0), 3: lambda: begin(g1, d0), 4: lambda: sums.step(0, d1), 5: lambda: sums.step(0, g0), 6: lambda: begin(u0, g1)}
     gates.run(va, hooks.items())
     sums.begin([u1])
     sums.step(1, g0, d0, g1)
@@ -828,7 +819,7 @@
     weights = [pltpu.with_memory_space_constraint(w, pltpu.HBM) for w in weights]
     flip = lambda k, t: t if k % 3 == 2 else jnp.swapaxes(t, 0, 1)
     moments = [flip(k, t) for k, t in enumerate(moments)]
-    outs = [out(t.shape, F32) for t in moments] + [vmem((PAIR * L, 16, FF), BF), vmem((L, DROWS, D), BF)]
+    outs = [out(t.shape, F32) for t in moments] + [out((PAIR * L, 16, FF), BF), vmem((L, DROWS, D), BF)]
     scratch = [vmem((PAIR * L, 16, FF), BF), vmem((L, DROWS, D), BF)] + [vmem((ROWS, L, FF), F32)] * 2 + [dma((PAIR * L + 1,))]
     *new, ng, nd = call(adamw_kernel, outs, [VM] * 11 + [HBM] * 3, scratch, "adamw", MOST - 5 * 2**17, out_specs=[VM] * 8)(*sums, norm, *moments, *weights)
     return [flip(k, t) for k, t in enumerate(new)], ng, nd
@@ -972,36 +963,37 @@
     n, sems = PAIR * L, PHASES * 4 + RING
     scratch = [vmem((ZROWS, HG), F32), vmem((n, 16, HG), BF), vmem((RING, ZROWS, HG), BF), vmem((n, ZROWS, GATE.width), F32), vmem((ZROWS, GATE.width), F32)]
     scratch += [dma((n + L,))] * 2 + [dma((2, 4))] * 2 + [dma((n, 2, sems))] * 2 + [dma((L, 2, sems))] * 2
-    return call(ag_kernel, outs, [VM] * 2, scratch, "ag", vmem_limit=5 * 2**20, ident=3, out_specs=[VM] * 3)(wg, wd)
-
-
-def put_kernel(src, dst, sem):
-    copies = [pltpu.make_async_copy(src.at[l, x], dst.at[l, x], sem.at[l, x]) for l in BOTH for x in range(RING)]
-    for cp in copies:
-        cp.start()
-    for cp in copies:
+    return call(ag_kernel, outs, [VM] * 2, scratch, "ag", vmem_limit=3 * 2**20, ident=3, out_specs=[VM] * 3)(wg, wd)
+
+
+def put_kernel(*refs):
+    *refs, sem = refs
+    n = len(refs) // 2
+    pairs = [(refs[k].at[l, x], refs[n + k].at[l, x]) for k in range(n) for l in BOTH for x in range(RING)]
+    for cp in fetch(pairs, sem):
         cp.wait()
 
 
-def put(w):
-    return call(put_kernel, [out(w.shape, BF)], [VM], [dma((L, RING))], "put", vmem_limit=2**20)(w)[0]
+def put(weights):
+    n = len(weights)
+    return call(put_kernel, [out(w.shape, BF) for w in weights], [VM] * n, [dma((n * L * RING,))], "put", vmem_limit=2**20)(*weights)
 
 
 def device_step(x, dy, wg, wu, wd, *moments):
     x, dy = x[0], dy[0]
-    a0, hid0, by_gate, by_up, h1, a1, hid1, d1 = forward(x, dy, wg, wu, wd)
-    d0, pd0, gg1, gd1, squares1 = back(d1, h1, dy, wg, wu, wd, by_gate, by_up, hid0, *dw(a1, d1, hid1, dy))
+    a0, hid0, by_gate, by_up, h1, d1, pg1, pd1 = forward(x, dy, wg, wu, wd)
+    d0, pd0, gg1, gd1, squares1 = back(d1, h1, dy, wg, wu, wd, by_gate, by_up, hid0, pg1, pd1)
     gg0, gd0, norm = end(a0, d0, pd0, squares1)
     moments, ng, nd = adamw((gg0, gg1, gd0, gd1), norm, moments, (wg, wu, wd))
-    return (*(put(new).reshape(w.shape) for new, w in zip(ag(ng, nd), (wg, wu, wd))), *moments)
+    return (*(new.reshape(w.shape) for new, w in zip(put(ag(ng, nd)), (wg, wu, wd))), *moments)
 
 
 def solution(mesh):
-    rows, moment, whole = P(("rep", "dp"), None, None), P(None, "dp", None), P(None, None, None)
+    rows, moment, whole = P(("rep", "dp")), P(None, "dp"), P()
     return jax.shard_map(
         device_step,
         mesh=mesh,
         in_specs=(rows,) * 2 + (whole,) * 3 + (moment,) * 6,
-        out_specs=(P("rep", None, None),) * 3 + (P("rep", "dp", None),) * 6,
+        out_specs=(P("rep"),) * 3 + (P("rep", "dp"),) * 6,
         check_vma=False,
     )

time: 414 us -> 406 us (0.981)
  Pallas kernels: 412 us -> 404 us
    pallas_call x6 -> x3, Pallas kernels: 242 us -> 238 us  [the longest x1 113 us: ag(): call(ag_kernel, outs, [VM] * 2, scratch, 'ag', vmem_limit=3 * 2 ** 20, id...]
where the time goes in v3:
time: 406 us
  Pallas kernels  404 us (100%)
    pallas_call x1, Pallas kernels, ag(): call(ag_kernel, outs, [VM] * 2, scratch, 'ag', vmem_limit=3 * 2 ** 20, id...  113 us
    pallas_call x1, Pallas kernels, forward(): call(forward_kernel, outs, [HBM] * 5, scratch, 'forward', ident=1)  110 us
    pallas_call x1, Pallas kernels, end(): call(end_kernel, ROWS_OUT, [HBM] * 4, scratch, 'end', ident=4)  83.1 us
    pallas_call x1, Pallas kernels, back(): call(back_kernel, outs, [HBM] * len(args), scratch, 'back', ident=2)  77.9 us
    pallas_call x1, Pallas kernels, put(): call(put_kernel, [out(w.shape, BF) for w in weights], [VM] * n, [dma((n *...  15.2 us

profile of v3, /device:TPU:1, one launch (start us, length us, event | category | flops | bytes accessed | tf_op | source)
XLA Modules:
  0.0 405.6 jit_solution(6863896616099518128)
XLA Ops:
  0.6 109.6 %forward.1 = (bf16[1024,1280]{1,0:T(8,128)(2,1)}, bf16[1024,3072]{1,0:T(8,128)(2,1)}, f32[1024,3072]{1,0:T(8,128)}, f32[1024,3072]{1,0:T(8,128)}, bf16[1024,1280...) custom-call(bf16[1024,1280]{1,0:T(8,128)(2,1)} %bitcast.19, ...), custom_call_target="tpu_custom_call" | custom-call | tf_op jit(solution)/shard_map/forward/pallas_call | solution.py:408
  110.2 77.9 %back.1 = (bf16[2,1024,3072]{2,1,0:T(8,128)(2,1)}, bf16[3,3072,640]{2,1,0:T(8,128)(2,1)}, bf16[2,16,3072]{2,1,0:T(8,128)(2,1)}, bf16[24,1280]{1,0:T(8,128)(2,1)}, f32[8,128]{1,0:T(8,128)}) custom-call(bf16[2,1024,3072]{2,1,0:T(8,128)(2,1)} %get-tuple-element.40.d, bf16[1024,1280]{1,0:T(8,128)(2,1)} %get-tuple-element.41.h1, bf16[1024,1280]{1,0:T(8,128)(2,1)} %bitcast.18, ...), custom_call_target="tpu_custom_call" | custom-call | tf_op jit(solution)/shard_map/back/pallas_call | solution.py:735
  188.1 83.1 %end.1 = (bf16[2,16,3072]{2,1,0:T(8,128)(2,1)}, bf16[24,1280]{1,0:T(8,128)(2,1)}, f32[8,128]{1,0:T(8,128)}) custom-call(bf16[1024,1280]{1,0:T(8,128)(2,1)} %get-tuple-element.39.a, bf16[2,1024,3072]{2,1,0:T(8,128)(2,1)} %get-tuple-element.47.d, bf16[3,4,4,4,2,24,640]{6,5,4,3,2,1,0:T(8,128)(2,1)} %bitcast.15, f32[8,128]{1,0:T(8,128)} %get-tuple-element.49.sq), custom_call_target="tpu_custom_call" | custom-call | tf_op jit(solution)/shard_map/end/pallas_call | solution.py:779
  271.2 5.2 %adamw.1 = (f32[10,2,3072]{2,1,0:T(2,128)}, f32[10,2,3072]{2,1,0:T(2,128)}, f32[2,24,1280]{2,1,0:T(8,128)}, f32[10,2,3072]{2,1,0:T(2,128)}, f32[10,2,3072]{2,1,0...) custom-call(bf16[2,16,3072]{2,1,0:T(8,128)(2,1)} %get-tuple-element.50.gg0, ...), custom_call_target="tpu_custom_call" | custom-call | tf_op jit(solution)/shard_map/adamw/pallas_call | solution.py:824
  276.4 0.0 copy-start
  276.4 1.0 copy-done
  277.4 112.7 %ag.1 = (bf16[2,4,4,1,80,3072]{5,4,3,2,1,0:T(8,128)(2,1)S(1)}, bf16[2,4,4,1,80,3072]{5,4,3,2,1,0:T(8,128)(2,1)S(1)}, bf16[2,4,4,4,2,24,1280]{6,5,4,3,2,1,0:T(8,128)(2,1)S(1)}) custom-call(bf16[4,16,3072]{2,1,0:T(8,128)(2,1)S(1)} %copy-done, bf16[2,24,1280]{2,1,0:T(8,128)(2,1)S(1)} %get-tuple-element.56.wd), custom_call_target="tpu_custom_call" | custom-call | tf_op jit(solution)/shard_map/ag/pallas_call | solution.py:966
  390.1 15.2 %put.1 = (bf16[2,4,4,1,80,3072]{5,4,3,2,1,0:T(8,128)(2,1)}, bf16[2,4,4,1,80,3072]{5,4,3,2,1,0:T(8,128)(2,1)}, bf16[2,4,4,4,2,24,1280]{6,5,4,3,2,1,0:T(8,128)(2,1)}) custom-call(bf16[2,4,4,1,80,3072]{5,4,3,2,1,0:T(8,128)(2,1)S(1)} %get-tuple-element.57.refs_0_, bf16[2,4,4,1,80,3072]{5,4,3,2,1,0:T(8,128)(2,1)S(1)} %get-tuple-element.58.refs_1_, ...), custom_call_target="tpu_custom_call" | custom-call | tf_op jit(solution)/shard_map/put/pallas_call | solution.py:979
Async XLA Ops:
  276.4 1.0 copy-start

commit v4 on v3

--- a/solution.py
+++ b/solution.py
@@ -34,12 +34,12 @@
             steps += [lax.rem(steps[0] + r, RING) for r in range(1, RING)]
         self.peers = {}
 
-    def moved(self, dim, by=1):
+    def moved(self, dim, by=1, core=0):
         by %= len(self.at[dim])
-        if (dim, by) not in self.peers:
-            x, y, z, core = (steps[by if d == dim else 0] for d, steps in enumerate(self.at))
-            self.peers[dim, by] = {"dp": ((x * RING + y) * RING + z) * PAIR + core}
-        return self.peers[dim, by]
+        if (dim, by, core) not in self.peers:
+            x, y, z, c = (steps[by if d == dim else core if d == CORE else 0] for d, steps in enumerate(self.at))
+            self.peers[dim, by, core] = {"dp": ((x * RING + y) * RING + z) * PAIR + c}
+        return self.peers[dim, by, core]
 
 
 def meet(peers):
@@ -628,17 +628,22 @@
 DOWN_BLOCKS = (GOT + 1, RING, RING, RING, PAIR, DROWS, HD)
 
 
+def stages(here):
+    along = lambda d, core=0: [here.moved(d, r, core) for r in range(1, RING)]
+    return [here.moved(CORE)] + along(Z) + along(Z, 1), along(Y), along(X)
+
+
 def all_peers(here):
-    return [here.moved(d, r) for d in (X, Y, Z) for r in range(1, RING)] + [here.moved(CORE)]
+    return sum(stages(here), [])
 
 
 def over_all(here, total, nb, nr, send, recv):
     n = 0
-    for stage, dim in enumerate((CORE, Z, Y, X)):
+    for stage, peers in enumerate(stages(here)):
         nb[stage] = total
         copies = []
-        for r in range(1, len(here.at[dim])):
-            copies.append(remote(nb.at[stage], nr.at[n], send.at[n], recv.at[n], here.moved(dim, r)))
+        for peer in peers:
+            copies.append(remote(nb.at[stage], nr.at[n], send.at[n], recv.at[n], peer))
             copies[-1].start()
             n += 1
         for i, cp in enumerate(copies):
@@ -774,7 +779,7 @@
 
 
 def end(a, d, pd, sq):
-    scratch = [STATES, LANES, vmem((5, 8, 128), F32), vmem((10, 8, 128), F32)] + [dma((10,))] * 2 + [PAIR_SEM]
+    scratch = [STATES, LANES, vmem((5, 8, 128), F32), vmem((13, 8, 128), F32)] + [dma((13,))] * 2 + [PAIR_SEM]
     scratch += COLUMNS + GATE_SCRATCH + sums_scratch(True)
     return call(end_kernel, ROWS_OUT, [HBM] * 4, scratch, "end", ident=4)(a, d, pd.reshape(DOWN_BLOCKS), sq)
 
@@ -920,6 +925,8 @@
             zcopy(s, 2 + k).start()
     for st in down:
         st.forward(0)
+    for st in down:
+        st.end(0)
 
     for s in BOTH:
         cols = slice(s * GATE.width, (s + 1) * GATE.width)
@@ -933,8 +940,6 @@
         for st in gate[s::2]:
             (o0, o1)[st.u // L][st.u % L, x, y, 0, :, st.whole[0]] = zf[st.u].astype(BF)
             st.start(1)
-    for st in down:
-        st.end(0)
     both = gate[: L * 2] + down[:2] + gate[L * 2 :] + down[2:]
     for phase in (1, 2):
         for st in both:

time: 406 us -> 406 us (level)
  no operation moved by 1% of the time
where the time goes in v4:
time: 406 us; the launch traced here: 405 us
  Pallas kernels  403 us (99%)
    pallas_call x1, Pallas kernels, ag(): call(ag_kernel, outs, [VM] * 2, scratch, 'ag', vmem_limit=3 * 2 ** 20, id...  112 us
    pallas_call x1, Pallas kernels, forward(): call(forward_kernel, outs, [HBM] * 5, scratch, 'forward', ident=1)  110 us
    pallas_call x1, Pallas kernels, end(): call(end_kernel, ROWS_OUT, [HBM] * 4, scratch, 'end', ident=4)  83.1 us
    pallas_call x1, Pallas kernels, back(): call(back_kernel, outs, [HBM] * len(args), scratch, 'back', ident=2)  77.9 us
    pallas_call x1, Pallas kernels, put(): call(put_kernel, [out(w.shape, BF) for w in weights], [VM] * n, [dma((n *...  15.2 us

profile of v4, /device:TPU:1, one launch (start us, length us, event | category | flops | bytes accessed | tf_op | source)
XLA Modules:
  0.0 405.0 jit_solution(303688825517716490)
XLA Ops:
  0.6 109.6 %forward.1 = (bf16[1024,1280]{1,0:T(8,128)(2,1)}, bf16[1024,3072]{1,0:T(8,128)(2,1)}, f32[1024,3072]{1,0:T(8,128)}, f32[1024,3072]{1,0:T(8,128)}, bf16[1024,1280...) custom-call(bf16[1024,1280]{1,0:T(8,128)(2,1)} %bitcast.19, ...), custom_call_target="tpu_custom_call" | custom-call | tf_op jit(solution)/shard_map/forward/pallas_call | solution.py:408
  110.2 77.9 %back.1 = (bf16[2,1024,3072]{2,1,0:T(8,128)(2,1)}, bf16[3,3072,640]{2,1,0:T(8,128)(2,1)}, bf16[2,16,3072]{2,1,0:T(8,128)(2,1)}, bf16[24,1280]{1,0:T(8,128)(2,1)}, f32[8,128]{1,0:T(8,128)}) custom-call(bf16[2,1024,3072]{2,1,0:T(8,128)(2,1)} %get-tuple-element.40.d, bf16[1024,1280]{1,0:T(8,128)(2,1)} %get-tuple-element.41.h1, bf16[1024,1280]{1,0:T(8,128)(2,1)} %bitcast.18, ...), custom_call_target="tpu_custom_call" | custom-call | tf_op jit(solution)/shard_map/back/pallas_call | solution.py:740
  188.2 83.1 %end.1 = (bf16[2,16,3072]{2,1,0:T(8,128)(2,1)}, bf16[24,1280]{1,0:T(8,128)(2,1)}, f32[8,128]{1,0:T(8,128)}) custom-call(bf16[1024,1280]{1,0:T(8,128)(2,1)} %get-tuple-element.39.a, bf16[2,1024,3072]{2,1,0:T(8,128)(2,1)} %get-tuple-element.47.d, bf16[3,4,4,4,2,24,640]{6,5,4,3,2,1,0:T(8,128)(2,1)} %bitcast.15, f32[8,128]{1,0:T(8,128)} %get-tuple-element.49.sq), custom_call_target="tpu_custom_call" | custom-call | tf_op jit(solution)/shard_map/end/pallas_call | solution.py:784
  271.3 5.2 %adamw.1 = (f32[10,2,3072]{2,1,0:T(2,128)}, f32[10,2,3072]{2,1,0:T(2,128)}, f32[2,24,1280]{2,1,0:T(8,128)}, f32[10,2,3072]{2,1,0:T(2,128)}, f32[10,2,3072]{2,1,0...) custom-call(bf16[2,16,3072]{2,1,0:T(8,128)(2,1)} %get-tuple-element.50.gg0, ...), custom_call_target="tpu_custom_call" | custom-call | tf_op jit(solution)/shard_map/adamw/pallas_call | solution.py:829
  276.5 0.0 copy-start
  276.5 1.0 copy-done
  277.5 112.0 %ag.1 = (bf16[2,4,4,1,80,3072]{5,4,3,2,1,0:T(8,128)(2,1)S(1)}, bf16[2,4,4,1,80,3072]{5,4,3,2,1,0:T(8,128)(2,1)S(1)}, bf16[2,4,4,4,2,24,1280]{6,5,4,3,2,1,0:T(8,128)(2,1)S(1)}) custom-call(bf16[4,16,3072]{2,1,0:T(8,128)(2,1)S(1)} %copy-done, bf16[2,24,1280]{2,1,0:T(8,128)(2,1)S(1)} %get-tuple-element.56.wd), custom_call_target="tpu_custom_call" | custom-call | tf_op jit(solution)/shard_map/ag/pallas_call | solution.py:971
  389.5 15.2 %put.1 = (bf16[2,4,4,1,80,3072]{5,4,3,2,1,0:T(8,128)(2,1)}, bf16[2,4,4,1,80,3072]{5,4,3,2,1,0:T(8,128)(2,1)}, bf16[2,4,4,4,2,24,1280]{6,5,4,3,2,1,0:T(8,128)(2,1)}) custom-call(bf16[2,4,4,1,80,3072]{5,4,3,2,1,0:T(8,128)(2,1)S(1)} %get-tuple-element.57.refs_0_, bf16[2,4,4,1,80,3072]{5,4,3,2,1,0:T(8,128)(2,1)S(1)} %get-tuple-element.58.refs_1_, ...), custom_call_target="tpu_custom_call" | custom-call | tf_op jit(solution)/shard_map/put/pallas_call | solution.py:984
Async XLA Ops:
  276.5 1.0 copy-start
